TPU v7x, 32 devices: a whole 2x2x4 slice. The times are simulated.
32 devices in a mesh: dp: 2 (over y), fsdp: 4 (over z), tensor: 4 (over x, core).
Axes of the slice: x: 2, y: 2, z: 4, core: 2. Of those that a mesh axis runs over, the one named last changes fastest.
Arguments:
- tokens: bfloat16 [2048, 8192], P(('dp', 'fsdp')), may hold values from -40 to 40
- next_tokens: bfloat16 [2048, 8192], P(('dp', 'fsdp')), may hold values from -6 to 6
- cotangent: bfloat16 [2, 2048, 1024], P(None, ('dp', 'fsdp'), 'tensor'), may hold values from -6 to 6
- master: float32 [2, 8192, 1024], P(None, 'fsdp', 'tensor'), may hold values from -0.0625 to 0.0625
- first_moment: float32 [2, 8192, 1024], P(None, 'fsdp', 'tensor'), may hold values from -6 to 6
- second_moment: float32 [2, 8192, 1024], P(None, 'fsdp', 'tensor'), may hold values from 0.25 to 4
Outputs:
- new_master: float32 [2, 8192, 1024], P(None, 'fsdp', 'tensor')
- new_first: float32 [2, 8192, 1024], P(None, 'fsdp', 'tensor')
- new_second: float32 [2, 8192, 1024], P(None, 'fsdp', 'tensor')
- projected: bfloat16 [2, 2048, 1024], P(None, ('dp', 'fsdp'), 'tensor')
All inputs are finite; a program needn't handle non-finite values.
Results may differ from a plain program's by a relative error of at most 0.005.
Values may be sent and summed in bfloat16 or wider, within the bound.
No kernel may reach another device: no remote copies, remote signals or barrier semaphores. Data moves between devices by JAX's collectives and lax.ppermute only.
A program may use at most 128 MiB of HBM per device.

v0:
```python
import functools

import jax
import jax.numpy as jnp
from jax import lax
from jax.experimental import pallas as pl
from jax.experimental.pallas import tpu as pltpu
from jax.sharding import PartitionSpec as P

STEP = 10
VMEM = pl.BlockSpec(memory_space=pltpu.VMEM)
SMEM = pl.BlockSpec(memory_space=pltpu.SMEM)


def shift(x, axis, k):
    n = lax.axis_size(axis)
    return lax.ppermute(x, axis, [(i, (i + k) % n) for i in range(n)])


def spread(x, axis):
    n = lax.axis_size(axis)
    pieces = {0: x}
    stride = n // 2
    while stride:
        for r, piece in list(pieces.items()):
            pieces[r ^ stride] = lax.ppermute(piece, axis, [(i, i ^ stride) for i in range(n)])
        stride //= 2
    return [pieces[r] for r in range(n)]


def contract_rows(a, b):
    return lax.dot_general(a, b, (((0,), (0,)), ((), ())), preferred_element_type=jnp.float32)


def row_blocks(refs, rows):
    return [ref[i : i + rows, :] for ref in refs for i in range(0, ref.shape[0], rows)]


def grad_kernel(n_f, n_t, own, groups, at_ref, *refs):
    tokens, cots, refs = refs[: groups * n_t], refs[groups * n_t : groups * n_t + n_f], refs[groups * n_t + n_f :]
    rows, chunk = cots[0].shape[1], tokens[0].shape[1]
    squares = jnp.zeros((8, 128), jnp.float32)
    for r in range(n_t):
        at = pl.multiple_of((at_ref[0] ^ r) * chunk, chunk)
        for s in range(2):
            blocks = row_blocks(tokens[r::n_t], rows)
            acc = functools.reduce(jnp.add, [contract_rows(b, c[s]) for b, c in zip(blocks, cots, strict=True)])
            if own:
                refs[0][s, pl.ds(at, chunk), :] = acc
            else:
                acc += refs[0][s, pl.ds(at, chunk), :]
                refs[1][s, pl.ds(at, chunk), :] = acc
                squares += jnp.sum((acc * acc).reshape(-1, 8, 128), axis=0)
    if not own:
        refs[2][...] = squares


def clip_scale(squares, count):
    total = jnp.sum(squares)
    return jnp.minimum(1.0, 1.0 / jnp.sqrt(jnp.full((8, 128), total / count, jnp.float32) + 1e-06))[:1, :1]


def adam_update(scale, grad, master, first_moment, second_moment):
    clipped = scale * grad
    new_first = 0.9 * first_moment + 0.1 * clipped
    new_second = 0.95 * second_moment + 0.05 * clipped * clipped
    first_hat = new_first / (1.0 - 0.9**STEP)
    second_hat = new_second / (1.0 - 0.95**STEP)
    new_master = master - 0.003 * (first_hat / (jnp.sqrt(second_hat) + 1e-08) + 0.1 * master)
    return (new_master, new_first, new_second)


def project_kernel(n_f, n_t, groups, count, at_ref, squares_ref, grad_ref, master_ref, m_ref, v_ref, own_ref, *refs):
    rest, outs, weight = refs[: groups * n_t], refs[groups * n_t : -1], refs[-1]
    rows, chunk = own_ref.shape[0], rest[0].shape[1]
    s, b = pl.program_id(0), pl.program_id(1)
    scale = clip_scale(squares_ref[...], count)
    new_master, _, _ = adam_update(scale, grad_ref[0], master_ref[0], m_ref[0], v_ref[0])
    block = new_master.shape[0]
    weight[s, pl.ds(pl.multiple_of(b * block, block), block), :] = new_master.astype(jnp.bfloat16)

    @pl.when((s == 1) & (b == pl.num_programs(1) - 1))
    def _():
        for s in range(2):
            outs[0][s] = jnp.dot(own_ref[...], weight[s], preferred_element_type=jnp.float32)
            blocks = [row_blocks(rest[r::n_t], rows) for r in range(n_t)]
            for k in range(1, n_f):
                acc = jnp.zeros(outs[0].shape[1:], jnp.float32)
                for r in range(n_t):
                    at = pl.multiple_of((at_ref[0] ^ r) * chunk, chunk)
                    acc += jnp.dot(
                        blocks[r][k - 1], weight[s, pl.ds(at, chunk), :], preferred_element_type=jnp.float32
                    )
                outs[k][s] = acc.astype(jnp.bfloat16)


def update_kernel(count, squares_ref, grad_ref, master_ref, m_ref, v_ref, new_master_ref, new_m_ref, new_v_ref):
    scale = clip_scale(squares_ref[...], count)
    new_master_ref[...], new_m_ref[...], new_v_ref[...] = adam_update(
        scale.reshape(1, 1, 1), grad_ref[...], master_ref[...], m_ref[...], v_ref[...]
    )


def per_device(tokens, next_tokens, cotangent, master, first_moment, second_moment):
    n_f, n_t = lax.axis_size("fsdp"), lax.axis_size("tensor")
    f, t = lax.axis_index("fsdp"), lax.axis_index("tensor")
    rows, width = tokens.shape
    shard = width // n_f
    chunk = shard // n_t
    kv = cotangent.shape[2]
    count = 2.0 * width * kv * n_t
    at = t.reshape(1).astype(jnp.int32)

    def mine(x, owner, r=0):
        return lax.dynamic_slice(x, (0, owner * shard + (t ^ r) * chunk), (rows, chunk))

    def fetch(x):
        return [shift(mine(x, (f + k) % n_f), "fsdp", k) for k in range(1, n_f)]

    def flat(groups):
        return [piece for group in groups for piece in group]

    first = [mine(tokens, f, r) for r in range(n_t)]
    rest = jnp.concatenate(fetch(tokens), axis=0)
    other_first = spread(shift(first[0], "dp", 1), "tensor")
    other_rest = spread(shift(rest, "dp", 1), "tensor")
    rest = spread(rest, "tensor")
    cots = [cotangent] + [shift(cotangent, "fsdp", k) for k in range(1, n_f)]
    other_cots = [shift(c, "dp", 1) for c in cots]
    next_block = lax.dynamic_slice(next_tokens, (0, f * shard), (rows, shard))
    next_rest = [spread(x, "tensor") for x in fetch(next_tokens)]

    shard_type = jax.ShapeDtypeStruct((2, shard, kv), jnp.float32)
    grad = pl.pallas_call(
        functools.partial(grad_kernel, n_f, n_t, True, 2),
        out_shape=shard_type,
        in_specs=[SMEM] + [VMEM] * (2 * n_t + n_f),
        out_specs=VMEM,
    )(at, *first, *rest, *cots)
    grad, squares = pl.pallas_call(
        functools.partial(grad_kernel, n_f, n_t, False, 2),
        out_shape=(shard_type, jax.ShapeDtypeStruct((8, 128), jnp.float32)),
        in_specs=[SMEM] + [VMEM] * (2 * n_t + n_f + 1),
        out_specs=(VMEM, VMEM),
    )(at, *other_first, *other_rest, *other_cots, grad)

    for axis, n in (("fsdp", n_f), ("tensor", n_t)):
        squares = functools.reduce(jnp.add, [shift(squares, axis, k) for k in range(1, n)], squares)

    block = min(shard, 512)
    tile = pl.BlockSpec((1, block, kv), lambda s, b: (s, b, 0))
    whole = pl.BlockSpec(memory_space=pltpu.VMEM)
    out = (2, rows, kv)
    partial = pl.pallas_call(
      functools.partial(project_kernel, n_f, n_t, n_f - 1, count),
      grid=(2, shard // block),
      out_shape=(jax.ShapeDtypeStruct(out, jnp.float32),) + (jax.ShapeDtypeStruct(out, jnp.bfloat16),) * (n_f - 1),
      in_specs=[SMEM, whole] + [tile] * 4 + [whole] * (1 + (n_f - 1) * n_t),
      out_specs=(whole,) * n_f,
      scratch_shapes=[pltpu.VMEM((2, shard, kv), jnp.bfloat16)],
    )(at, squares, grad, master, first_moment, second_moment, next_block, *flat(next_rest))
    got = [shift(partial[k], "fsdp", -k) for k in range(1, n_f)]
    projected = functools.reduce(jnp.add, [g.astype(jnp.float32) for g in got], partial[0])
    new_master, new_first, new_second = pl.pallas_call(
      functools.partial(update_kernel, count),
      grid=(2, shard // block),
      out_shape=(shard_type,) * 3,
      in_specs=[whole] + [tile] * 4,
      out_specs=(tile,) * 3,
    )(squares, grad, master, first_moment, second_moment)
    return (new_master, new_first, new_second, projected.astype(jnp.bfloat16))


def solution(mesh):
    in_specs = (
        P(("dp", "fsdp"), None),
        P(("dp", "fsdp"), None),
        P(None, ("dp", "fsdp"), "tensor"),
        P(None, "fsdp", "tensor"),
        P(None, "fsdp", "tensor"),
        P(None, "fsdp", "tensor"),
    )
    out_specs = (
        P(None, "fsdp", "tensor"),
        P(None, "fsdp", "tensor"),
        P(None, "fsdp", "tensor"),
        P(None, ("dp", "fsdp"), "tensor"),
    )
    return jax.shard_map(per_device, mesh=mesh, in_specs=in_specs, out_specs=out_specs, check_vma=False)
```

profile of v0, /device:TPU:0, one launch (start us, length us, event | category | flops | bytes accessed | tf_op | source)
XLA Modules:
  0.0 195.9 jit_solution(5930401905281499097)
XLA Ops:
  0.7 2.4 %constant_dynamic-slice_fusion.4 = (bf16[256,512]{1,0:T(8,128)(2,1)}, bf16[256,512]{1,0:T(8,128)(2,1)}, bf16[256,512]{1,0:T(8,128)(2,1)S(1)}, bf16[256,512]{1,0:...) fusion(bf16[256,8192]{1,0:T(8,128)(2,1)} %param.6, ...), kind=kLoop, calls=%fused_computation.10 | loop fusion | bytes 3670044 | tf_op jit(solution)/shard_map/dynamic_slice | solution.py:115
  3.1 3.1 %collective-permute-start.4 = (bf16[256,512]{1,0:T(8,128)(2,1)S(1)}, bf16[256,512]{1,0:T(8,128)(2,1)S(1)}, u32[]{:S(2)}, u32[]{:S(2)}) collective-permute-start(bf16[256,512]{1,0:T(8,128)(2,1)S(1)} %get-tuple-element.29), channel_id=1, source_target_pairs={{0,4},{4,8},{8,12},{12,0},{1,5},{5,9},{9,13},{13,1},{2,6},{6,10},{... | collective-permute-start | bytes 786440 | tf_op jit(solution)/shard_map/ppermute | solution.py:17
  6.1 2.6 %collective-permute-start.5 = (bf16[256,512]{1,0:T(8,128)(2,1)S(1)}, bf16[256,512]{1,0:T(8,128)(2,1)S(1)}, u32[]{:S(2)}, u32[]{:S(2)}) collective-permute-start(bf16[256,512]{1,0:T(8,128)(2,1)S(1)} %get-tuple-element.28), channel_id=1, source_target_pairs={{0,8},{4,12},{8,0},{12,4},{1,9},{5,13},{9,1},{13,5},{2,10},{6,14},... | collective-permute-start | bytes 786440 | tf_op jit(solution)/shard_map/ppermute | solution.py:17
  8.7 1.3 collective-permute-start.6
  10.1 5.4 %collective-permute-done.4 = bf16[256,512]{1,0:T(8,128)(2,1)S(1)} collective-permute-done((bf16[256,512]{1,0:T(8,128)(2,1)S(1)}, bf16[256,512]{1,0:T(8,128)(2,1)S(1)}, u32[]{:S(2)}, u32[]{:S(2)}) %collective-permute-start.4) | collective-permute-done | bytes 262176 | tf_op jit(solution)/shard_map/ppermute | solution.py:17
  15.5 10.4 %collective-permute-done.5 = bf16[256,512]{1,0:T(8,128)(2,1)S(1)} collective-permute-done((bf16[256,512]{1,0:T(8,128)(2,1)S(1)}, bf16[256,512]{1,0:T(8,128)(2,1)S(1)}, u32[]{:S(2)}, u32[]{:S(2)}) %collective-permute-start.5) | collective-permute-done | bytes 262176 | tf_op jit(solution)/shard_map/ppermute | solution.py:17
  25.9 1.6 collective-permute-start.7
  27.5 6.1 %collective-permute-start.12 = (bf16[2,256,256]{2,1,0:T(8,128)(2,1)}, bf16[2,256,256]{2,1,0:T(8,128)(2,1)S(1)}, u32[]{:S(2)}, u32[]{:S(2)}) collective-permute-start(bf16[2,256,256]{2,1,0:T(8,128)(2,1)} %refs_8_.1), channel_id=1, source_target_pairs={{0,4},{4,8},{8,12},{12,0},{1,5},{5,9},{9,13},{13,1},{2,6},{6,10},{... | collective-permute-start | bytes 786440 | tf_op jit(solution)/shard_map/ppermute | solution.py:17
  33.6 1.6 collective-permute-start.14
  35.2 0.7 collective-permute-start.16
  35.9 0.5 collective-permute-start
  36.4 5.7 %collective-permute-done.12.refs_9_ = bf16[2,256,256]{2,1,0:T(8,128)(2,1)S(1)} collective-permute-done((bf16[2,256,256]{2,1,0:T(8,128)(2,1)}, bf16[2,256,256]{2,1,0:T(8,128)(2,1)S(1)}, u32[]{:S(2)}, u32[]{:S(2)}) %collective-permute-start.12) | collective-permute-done | bytes 262176 | tf_op jit(solution)/shard_map/ppermute | solution.py:17
  42.1 0.5 collective-permute-start.11
  42.6 8.7 %collective-permute-done.14.refs_10_ = bf16[2,256,256]{2,1,0:T(8,128)(2,1)S(1)} collective-permute-done((bf16[2,256,256]{2,1,0:T(8,128)(2,1)}, bf16[2,256,256]{2,1,0:T(8,128)(2,1)S(1)}, u32[]{:S(2)}, u32[]{:S(2)}) %collective-permute-start.14) | collective-permute-done | bytes 262176 | tf_op jit(solution)/shard_map/ppermute | solution.py:17
  51.4 1.5 collective-permute-start.19
  52.9 0.5 collective-permute-start.9
  53.4 1.2 constant_dynamic-slice_fusion
  54.6 5.2 %collective-permute-start.27 = (bf16[256,512]{1,0:T(8,128)(2,1)S(1)}, bf16[256,512]{1,0:T(8,128)(2,1)}, u32[]{:S(2)}, u32[]{:S(2)}) collective-permute-start(bf16[256,512]{1,0:T(8,128)(2,1)S(1)} %get-tuple-element.23), channel_id=1, source_target_pairs={{0,4},{4,8},{8,12},{12,0},{1,5},{5,9},{9,13},{13,1},{2,6},{6,10},{... | collective-permute-start | bytes 786440 | tf_op jit(solution)/shard_map/ppermute | solution.py:17
  59.7 3.3 %collective-permute-start.31 = (bf16[256,512]{1,0:T(8,128)(2,1)S(1)}, bf16[256,512]{1,0:T(8,128)(2,1)}, u32[]{:S(2)}, u32[]{:S(2)}) collective-permute-start(bf16[256,512]{1,0:T(8,128)(2,1)S(1)} %get-tuple-element.24), channel_id=1, source_target_pairs={{0,8},{4,12},{8,0},{12,4},{1,9},{5,13},{9,1},{13,5},{2,10},{6,14},... | collective-permute-start | bytes 786440 | tf_op jit(solution)/shard_map/ppermute | solution.py:17
  63.0 6.8 %collective-permute-done.27.refs_0_ = bf16[256,512]{1,0:T(8,128)(2,1)} collective-permute-done((bf16[256,512]{1,0:T(8,128)(2,1)S(1)}, bf16[256,512]{1,0:T(8,128)(2,1)}, u32[]{:S(2)}, u32[]{:S(2)}) %collective-permute-start.27) | collective-permute-done | bytes 262176 | tf_op jit(solution)/shard_map/ppermute | solution.py:17
  69.8 1.5 collective-permute-start.2
  71.3 7.7 %collective-permute-done.31.refs_4_ = bf16[256,512]{1,0:T(8,128)(2,1)} collective-permute-done((bf16[256,512]{1,0:T(8,128)(2,1)S(1)}, bf16[256,512]{1,0:T(8,128)(2,1)}, u32[]{:S(2)}, u32[]{:S(2)}) %collective-permute-start.31) | collective-permute-done | bytes 262176 | tf_op jit(solution)/shard_map/ppermute | solution.py:17
  79.0 0.5 collective-permute-start.13
  79.5 13.7 %collective-permute-done.2.refs_2_ = bf16[256,512]{1,0:T(8,128)(2,1)S(1)} collective-permute-done((bf16[256,512]{1,0:T(8,128)(2,1)S(1)}, bf16[256,512]{1,0:T(8,128)(2,1)S(1)}, u32[]{:S(2)}, u32[]{:S(2)}) %collective-permute-start.2) | collective-permute-done | bytes 262176 | tf_op jit(solution)/shard_map/ppermute | solution.py:26
  93.2 0.5 collective-permute-start.15
  93.7 0.5 collective-permute-start.20
  94.2 0.2 copy-done.20
  94.5 0.5 collective-permute-start.10
  95.0 5.5 %collective-permute-done.15.refs_10_ = bf16[2,256,256]{2,1,0:T(8,128)(2,1)S(1)} collective-permute-done((bf16[2,256,256]{2,1,0:T(8,128)(2,1)S(1)}, bf16[2,256,256]{2,1,0:T(8,128)(2,1)S(1)}, u32[]{:S(2)}, u32[]{:S(2)}) %collective-permute-start.15) | collective-permute-done | bytes 262176 | tf_op jit(solution)/shard_map/ppermute | solution.py:17
  100.5 0.5 collective-permute-start.17
  101.0 5.9 %collective-permute-done.17.refs_11_ = bf16[2,256,256]{2,1,0:T(8,128)(2,1)S(1)} collective-permute-done((bf16[2,256,256]{2,1,0:T(8,128)(2,1)S(1)}, bf16[2,256,256]{2,1,0:T(8,128)(2,1)S(1)}, u32[]{:S(2)}, u32[]{:S(2)}) %collective-permute-start.17) | collective-permute-done | bytes 262176 | tf_op jit(solution)/shard_map/ppermute | solution.py:17
  106.9 1.5 collective-permute-done.3.refs_3_
  108.5 1.5 collective-permute-start.29
  109.9 0.5 collective-permute-start.33
  110.5 1.5 collective-permute-start.37
  112.0 0.9 copy-done.5
  113.0 6.9 %shard_map.93.refs_12_ = f32[2,2048,256]{2,1,0:T(8,128)} custom-call(s32[1]{0:T(128)} %bitcast.at_ref, bf16[256,512]{1,0:T(8,128)(2,1)} %copy-done.1, bf16[256,512]{1,0:T(8,128)(2,1)} %get-tuple-element.26.refs_1_, bf16[256,512]{1,0:T(8,128)(2,1)} %get-tuple-element.31.refs_2_, bf16[256,512]{1,0:T(8,128)(2,1)} %get-tuple-element.25.refs_3_, ...), custom_call_target="tpu_custom_call" | custom-call | tf_op jit(solution)/shard_map/pallas_call | solution.py:134
  119.9 8.4 %shard_map.94 = (f32[2,2048,256]{2,1,0:T(8,128)}, f32[8,128]{1,0:T(8,128)}) custom-call(s32[1]{0:T(128)} %bitcast.at_ref, bf16[256,512]{1,0:T(8,128)(2,1)} %copy-done.14, bf16[256,512]{1,0:T(8,128)(2,1)} %copy-done.20, bf16[256,512]{1,0:T(8,128)(2,1)} %copy-done.19, bf16[256,512]{1,0:T(8,128)(2,1)} %copy-done.23, bf16[768,512]{1,0:T(8,128)(2,1)} %copy-done.2, ...), custom_call_target="tpu_custom_call" | custom-call | tf_op jit(solution)/shard_map/pallas_call | solution.py:140
  128.2 3.5 %collective-permute-start.21 = (f32[8,128]{1,0:T(8,128)}, f32[8,128]{1,0:T(8,128)S(1)}, u32[]{:S(2)}, u32[]{:S(2)}) collective-permute-start(f32[8,128]{1,0:T(8,128)} %get-tuple-element.13), channel_id=1, source_target_pairs={{0,4},{4,8},{8,12},{12,0},{1,5},{5,9},{9,13},{13,1},{2,6},{6,10},{... | collective-permute-start | bytes 12296 | tf_op jit(solution)/shard_map/ppermute | solution.py:17
  131.8 4.5 %collective-permute-done.21 = f32[8,128]{1,0:T(8,128)S(1)} collective-permute-done((f32[8,128]{1,0:T(8,128)}, f32[8,128]{1,0:T(8,128)S(1)}, u32[]{:S(2)}, u32[]{:S(2)}) %collective-permute-start.21) | collective-permute-done | bytes 4128 | tf_op jit(solution)/shard_map/ppermute | solution.py:17
  136.3 0.3 collective-permute-start.22
  136.6 4.4 %collective-permute-done.22 = f32[8,128]{1,0:T(8,128)S(1)} collective-permute-done((f32[8,128]{1,0:T(8,128)}, f32[8,128]{1,0:T(8,128)S(1)}, u32[]{:S(2)}, u32[]{:S(2)}) %collective-permute-start.22) | collective-permute-done | bytes 4128 | tf_op jit(solution)/shard_map/ppermute | solution.py:17
  141.0 2.0 %collective-permute-start.23 = (f32[8,128]{1,0:T(8,128)}, f32[8,128]{1,0:T(8,128)S(1)}, u32[]{:S(2)}, u32[]{:S(2)}) collective-permute-start(f32[8,128]{1,0:T(8,128)} %get-tuple-element.13), channel_id=1, source_target_pairs={{0,12},{4,0},{8,4},{12,8},{1,13},{5,1},{9,5},{13,9},{2,14},{6,2},{... | collective-permute-start | bytes 12296 | tf_op jit(solution)/shard_map/ppermute | solution.py:17
  143.0 1.8 collective-permute-done.23
  144.8 0.7 add_add_fusion.1
  145.5 0.6 collective-permute-start.25
  146.1 1.4 collective-permute-start.26
  147.5 0.5 collective-permute-start.36
  148.0 0.5 collective-permute-done.24
  148.5 0.6 collective-permute-done.25
  149.2 1.2 collective-permute-start.38
  150.4 2.3 %constant_dynamic-slice_fusion.3.own_ref = bf16[256,2048]{1,0:T(8,128)(2,1)} fusion(bf16[256,8192]{1,0:T(8,128)(2,1)} %param.7, s32[]{:T(128)S(6)} %select_n.58), kind=kLoop, calls=%fused_computation.9 | loop fusion | bytes 2097156 | tf_op jit(solution)/shard_map/dynamic_slice | solution.py:130
  152.7 0.6 add_add_fusion.squares_ref
  153.4 0.6 copy-done.9
  154.0 0.1 copy-done.10
  154.1 0.1 copy-done.11
  154.2 0.1 copy-done.12
  154.3 0.1 copy-done.13
  154.4 16.1 %shard_map.96 = (f32[2,256,256]{2,1,0:T(8,128)}, bf16[2,256,256]{2,1,0:T(8,128)(2,1)}, bf16[2,256,256]{2,1,0:T(8,128)(2,1)}, bf16[2,256,256]{2,1,0:T(8,128)(2,1)}) custom-call(s32[1]{0:T(128)} %bitcast.at_ref, f32[8,128]{1,0:T(8,128)} %add_add_fusion.squares_ref, f32[2,2048,256]{2,1,0:T(8,128)} %get-tuple-element.14.grad_ref, f32[2,2048,256]{2,1,0:T(8,128)} %master_ref.3, ...), custom_call_target="tpu_custom_call" | custom-call | tf_op jit(solution)/shard_map/pallas_call | solution.py:154
  170.5 3.9 %collective-permute-start.39 = (bf16[2,256,256]{2,1,0:T(8,128)(2,1)}, bf16[2,256,256]{2,1,0:T(8,128)(2,1)S(1)}, u32[]{:S(2)}, u32[]{:S(2)}) collective-permute-start(bf16[2,256,256]{2,1,0:T(8,128)(2,1)} %get-tuple-element.19), channel_id=1, source_target_pairs={{0,12},{4,0},{8,4},{12,8},{1,13},{5,1},{9,5},{13,9},{2,14},{6,2},{... | collective-permute-start | bytes 786440 | tf_op jit(solution)/shard_map/ppermute | solution.py:17
  174.3 0.6 collective-permute-start.41
  175.0 13.9 %shard_map.95 = (f32[2,2048,256]{2,1,0:T(8,128)}, f32[2,2048,256]{2,1,0:T(8,128)}, f32[2,2048,256]{2,1,0:T(8,128)}) custom-call(f32[8,128]{1,0:T(8,128)} %add_add_fusion.squares_ref, f32[2,2048,256]{2,1,0:T(8,128)} %get-tuple-element.14.grad_ref, f32[2,2048,256]{2,1,0:T(8,128)} %master_ref.3, f32[2,2048,256]{2,1,0:T(8,128)} %m_ref.3, f32[2,2048,256]{2,1,0:T(8,128)} %v_ref.3), custom_call_target="tpu_custom_call" | custom-call | tf_op jit(solution)/shard_map/pallas_call | solution.py:164
  188.9 6.1 %collective-permute-done.40 = bf16[2,256,256]{2,1,0:T(8,128)(2,1)S(1)} collective-permute-done((bf16[2,256,256]{2,1,0:T(8,128)(2,1)}, bf16[2,256,256]{2,1,0:T(8,128)(2,1)S(1)}, u32[]{:S(2)}, u32[]{:S(2)}) %collective-permute-start.40) | collective-permute-done | bytes 262176 | tf_op jit(solution)/shard_map/ppermute | solution.py:17
  195.0 0.8 add_convert_fusion
  (81 shorter events, 0.2 us)
Async XLA Ops:
  3.1 109.9 %copy-start.1 = (bf16[256,512]{1,0:T(8,128)(2,1)}, bf16[256,512]{1,0:T(8,128)(2,1)S(1)}, u32[]{:S(2)}) copy-start(bf16[256,512]{1,0:T(8,128)(2,1)S(1)} %get-tuple-element.30.refs_0_) | copy-start | bytes 786436
  3.1 12.4 %collective-permute-start.4 = (bf16[256,512]{1,0:T(8,128)(2,1)S(1)}, bf16[256,512]{1,0:T(8,128)(2,1)S(1)}, u32[]{:S(2)}, u32[]{:S(2)}) collective-permute-start(bf16[256,512]{1,0:T(8,128)(2,1)S(1)} %get-tuple-element.29), channel_id=1, source_target_pairs={{0,4},{4,8},{8,12},{12,0},{1,5},{5,9},{9,13},{13,1},{2,6},{6,10},{... | collective-permute-start | bytes 786440 | tf_op jit(solution)/shard_map/ppermute | solution.py:17
  6.1 19.7 %collective-permute-start.5 = (bf16[256,512]{1,0:T(8,128)(2,1)S(1)}, bf16[256,512]{1,0:T(8,128)(2,1)S(1)}, u32[]{:S(2)}, u32[]{:S(2)}) collective-permute-start(bf16[256,512]{1,0:T(8,128)(2,1)S(1)} %get-tuple-element.28), channel_id=1, source_target_pairs={{0,8},{4,12},{8,0},{12,4},{1,9},{5,13},{9,1},{13,5},{2,10},{6,14},... | collective-permute-start | bytes 786440 | tf_op jit(solution)/shard_map/ppermute | solution.py:17
  8.7 17.1 %collective-permute-start.6 = (bf16[256,512]{1,0:T(8,128)(2,1)S(1)}, bf16[256,512]{1,0:T(8,128)(2,1)S(1)}, u32[]{:S(2)}, u32[]{:S(2)}) collective-permute-start(bf16[256,512]{1,0:T(8,128)(2,1)S(1)} %get-tuple-element.27), channel_id=1, source_target_pairs={{0,12},{4,0},{8,4},{12,8},{1,13},{5,1},{9,5},{13,9},{2,14},{6,2},{... | collective-permute-start | bytes 786440 | tf_op jit(solution)/shard_map/ppermute | solution.py:17
  25.9 87.1 %copy-start = (bf16[768,512]{1,0:T(8,128)(2,1)}, bf16[768,512]{1,0:T(8,128)(2,1)S(1)}, u32[]{:S(2)}) copy-start(bf16[768,512]{1,0:T(8,128)(2,1)S(1)} %constant_dynamic-update-slice_fusion.refs_4_) | copy-start | bytes 2359300
  25.9 26.9 %collective-permute-start.7 = (bf16[768,512]{1,0:T(8,128)(2,1)S(1)}, bf16[768,512]{1,0:T(8,128)(2,1)S(1)}, u32[]{:S(2)}, u32[]{:S(2)}) collective-permute-start(bf16[768,512]{1,0:T(8,128)(2,1)S(1)} %constant_dynamic-update-slice_fusion.refs_4_), channel_id=1, source_target_pairs={{0,16},{16,0},{1,17},{17,1},{2,18},{18,2},{3,19},{19,3},{4,20},{20... | collective-permute-start | bytes 2359304 | tf_op jit(solution)/shard_map/ppermute | solution.py:17
  27.5 14.6 %collective-permute-start.12 = (bf16[2,256,256]{2,1,0:T(8,128)(2,1)}, bf16[2,256,256]{2,1,0:T(8,128)(2,1)S(1)}, u32[]{:S(2)}, u32[]{:S(2)}) collective-permute-start(bf16[2,256,256]{2,1,0:T(8,128)(2,1)} %refs_8_.1), channel_id=1, source_target_pairs={{0,4},{4,8},{8,12},{12,0},{1,5},{5,9},{9,13},{13,1},{2,6},{6,10},{... | collective-permute-start | bytes 786440 | tf_op jit(solution)/shard_map/ppermute | solution.py:17
  33.6 17.8 %collective-permute-start.14 = (bf16[2,256,256]{2,1,0:T(8,128)(2,1)}, bf16[2,256,256]{2,1,0:T(8,128)(2,1)S(1)}, u32[]{:S(2)}, u32[]{:S(2)}) collective-permute-start(bf16[2,256,256]{2,1,0:T(8,128)(2,1)} %refs_8_.1), channel_id=1, source_target_pairs={{0,8},{4,12},{8,0},{12,4},{1,9},{5,13},{9,1},{13,5},{2,10},{6,14},... | collective-permute-start | bytes 786440 | tf_op jit(solution)/shard_map/ppermute | solution.py:17
  35.2 19.4 %collective-permute-start.16 = (bf16[2,256,256]{2,1,0:T(8,128)(2,1)}, bf16[2,256,256]{2,1,0:T(8,128)(2,1)S(1)}, u32[]{:S(2)}, u32[]{:S(2)}) collective-permute-start(bf16[2,256,256]{2,1,0:T(8,128)(2,1)} %refs_8_.1), channel_id=1, source_target_pairs={{0,12},{4,0},{8,4},{12,8},{1,13},{5,1},{9,5},{13,9},{2,14},{6,2},{... | collective-permute-start | bytes 786440 | tf_op jit(solution)/shard_map/ppermute | solution.py:17
  35.9 23.8 %collective-permute-start = (bf16[256,512]{1,0:T(8,128)(2,1)S(1)}, bf16[256,512]{1,0:T(8,128)(2,1)S(1)}, u32[]{:S(2)}, u32[]{:S(2)}) collective-permute-start(bf16[256,512]{1,0:T(8,128)(2,1)S(1)} %get-tuple-element.30.refs_0_), channel_id=1, source_target_pairs={{0,16},{16,0},{1,17},{17,1},{2,18},{18,2},{3,19},{19,3},{4,20},{20... | collective-permute-start | bytes 786440 | tf_op jit(solution)/shard_map/ppermute | solution.py:17
  42.1 70.8 %copy-start.15 = (bf16[2,256,256]{2,1,0:T(8,128)(2,1)}, bf16[2,256,256]{2,1,0:T(8,128)(2,1)S(1)}, u32[]{:S(2)}) copy-start(bf16[2,256,256]{2,1,0:T(8,128)(2,1)S(1)} %collective-permute-done.12.refs_9_) | copy-start | bytes 786436
  42.1 20.9 %collective-permute-start.11 = (bf16[2,256,256]{2,1,0:T(8,128)(2,1)}, bf16[2,256,256]{2,1,0:T(8,128)(2,1)S(1)}, u32[]{:S(2)}, u32[]{:S(2)}) collective-permute-start(bf16[2,256,256]{2,1,0:T(8,128)(2,1)} %refs_8_.1), channel_id=1, source_target_pairs={{0,16},{16,0},{1,17},{17,1},{2,18},{18,2},{3,19},{19,3},{4,20},{20... | collective-permute-start | bytes 786440 | tf_op jit(solution)/shard_map/ppermute | solution.py:17
  51.4 61.5 %copy-start.16 = (bf16[2,256,256]{2,1,0:T(8,128)(2,1)}, bf16[2,256,256]{2,1,0:T(8,128)(2,1)S(1)}, u32[]{:S(2)}) copy-start(bf16[2,256,256]{2,1,0:T(8,128)(2,1)S(1)} %collective-permute-done.14.refs_10_) | copy-start | bytes 786436
  51.4 42.4 %collective-permute-start.19 = (bf16[768,512]{1,0:T(8,128)(2,1)S(1)}, bf16[768,512]{1,0:T(8,128)(2,1)S(1)}, u32[]{:S(2)}, u32[]{:S(2)}) collective-permute-start(bf16[768,512]{1,0:T(8,128)(2,1)S(1)} %constant_dynamic-update-slice_fusion.refs_4_), channel_id=1, source_target_pairs={{0,2},{1,3},{2,0},{3,1},{4,6},{5,7},{6,4},{7,5},{8,10},{9,11},{10,... | collective-permute-start | bytes 2359304 | tf_op jit(solution)/shard_map/ppermute | solution.py:26
  52.9 67.0 %copy-start.2 = (bf16[768,512]{1,0:T(8,128)(2,1)}, bf16[768,512]{1,0:T(8,128)(2,1)S(1)}, u32[]{:S(2)}) copy-start(bf16[768,512]{1,0:T(8,128)(2,1)S(1)} %collective-permute-done.7.refs_4_) | copy-start | bytes 2359300
  52.9 41.6 %collective-permute-start.9 = (bf16[768,512]{1,0:T(8,128)(2,1)S(1)}, bf16[768,512]{1,0:T(8,128)(2,1)S(1)}, u32[]{:S(2)}, u32[]{:S(2)}) collective-permute-start(bf16[768,512]{1,0:T(8,128)(2,1)S(1)} %collective-permute-done.7.refs_4_), channel_id=1, source_target_pairs={{0,2},{1,3},{2,0},{3,1},{4,6},{5,7},{6,4},{7,5},{8,10},{9,11},{10,... | collective-permute-start | bytes 2359304 | tf_op jit(solution)/shard_map/ppermute | solution.py:26
  54.6 58.3 %copy-start.18 = (bf16[2,256,256]{2,1,0:T(8,128)(2,1)}, bf16[2,256,256]{2,1,0:T(8,128)(2,1)S(1)}, u32[]{:S(2)}) copy-start(bf16[2,256,256]{2,1,0:T(8,128)(2,1)S(1)} %collective-permute-done.16.refs_11_) | copy-start | bytes 786436
  54.6 15.3 %collective-permute-start.27 = (bf16[256,512]{1,0:T(8,128)(2,1)S(1)}, bf16[256,512]{1,0:T(8,128)(2,1)}, u32[]{:S(2)}, u32[]{:S(2)}) collective-permute-start(bf16[256,512]{1,0:T(8,128)(2,1)S(1)} %get-tuple-element.23), channel_id=1, source_target_pairs={{0,4},{4,8},{8,12},{12,0},{1,5},{5,9},{9,13},{13,1},{2,6},{6,10},{... | collective-permute-start | bytes 786440 | tf_op jit(solution)/shard_map/ppermute | solution.py:17
  59.7 53.1 %copy-start.14 = (bf16[256,512]{1,0:T(8,128)(2,1)}, bf16[256,512]{1,0:T(8,128)(2,1)S(1)}, u32[]{:S(2)}) copy-start(bf16[256,512]{1,0:T(8,128)(2,1)S(1)} %collective-permute-done.refs_0_) | copy-start | bytes 786436
  59.7 19.3 %collective-permute-start.31 = (bf16[256,512]{1,0:T(8,128)(2,1)S(1)}, bf16[256,512]{1,0:T(8,128)(2,1)}, u32[]{:S(2)}, u32[]{:S(2)}) collective-permute-start(bf16[256,512]{1,0:T(8,128)(2,1)S(1)} %get-tuple-element.24), channel_id=1, source_target_pairs={{0,8},{4,12},{8,0},{12,4},{1,9},{5,13},{9,1},{13,5},{2,10},{6,14},... | collective-permute-start | bytes 786440 | tf_op jit(solution)/shard_map/ppermute | solution.py:17
  63.0 49.9 %copy-start.17 = (bf16[2,256,256]{2,1,0:T(8,128)(2,1)}, bf16[2,256,256]{2,1,0:T(8,128)(2,1)S(1)}, u32[]{:S(2)}) copy-start(bf16[2,256,256]{2,1,0:T(8,128)(2,1)S(1)} %collective-permute-done.11.refs_8_) | copy-start | bytes 786436
  63.0 16.0 %collective-permute-start.35 = (bf16[256,512]{1,0:T(8,128)(2,1)S(1)}, bf16[256,512]{1,0:T(8,128)(2,1)}, u32[]{:S(2)}, u32[]{:S(2)}) collective-permute-start(bf16[256,512]{1,0:T(8,128)(2,1)S(1)} %get-tuple-element.22), channel_id=1, source_target_pairs={{0,12},{4,0},{8,4},{12,8},{1,13},{5,1},{9,5},{13,9},{2,14},{6,2},{... | collective-permute-start | bytes 786440 | tf_op jit(solution)/shard_map/ppermute | solution.py:17
  69.8 23.4 %collective-permute-start.2 = (bf16[256,512]{1,0:T(8,128)(2,1)S(1)}, bf16[256,512]{1,0:T(8,128)(2,1)S(1)}, u32[]{:S(2)}, u32[]{:S(2)}) collective-permute-start(bf16[256,512]{1,0:T(8,128)(2,1)S(1)} %collective-permute-done.refs_0_), channel_id=1, source_target_pairs={{0,2},{1,3},{2,0},{3,1},{4,6},{5,7},{6,4},{7,5},{8,10},{9,11},{10,... | collective-permute-start | bytes 786440 | tf_op jit(solution)/shard_map/ppermute | solution.py:26
  79.0 14.7 %collective-permute-start.1 = (bf16[256,512]{1,0:T(8,128)(2,1)S(1)}, bf16[256,512]{1,0:T(8,128)(2,1)S(1)}, u32[]{:S(2)}, u32[]{:S(2)}) collective-permute-start(bf16[256,512]{1,0:T(8,128)(2,1)S(1)} %collective-permute-done.refs_0_), channel_id=1, source_target_pairs={{0,1},{1,0},{2,3},{3,2},{4,5},{5,4},{6,7},{7,6},{8,9},{9,8},{10,11... | collective-permute-start | bytes 786440 | tf_op jit(solution)/shard_map/ppermute | solution.py:26
  79.0 15.4 %collective-permute-start.13 = (bf16[2,256,256]{2,1,0:T(8,128)(2,1)S(1)}, bf16[2,256,256]{2,1,0:T(8,128)(2,1)}, u32[]{:S(2)}, u32[]{:S(2)}) collective-permute-start(bf16[2,256,256]{2,1,0:T(8,128)(2,1)S(1)} %collective-permute-done.12.refs_9_), channel_id=1, source_target_pairs={{0,16},{16,0},{1,17},{17,1},{2,18},{18,2},{3,19},{19,3},{4,20},{20... | collective-permute-start | bytes 786440 | tf_op jit(solution)/shard_map/ppermute | solution.py:17
  93.2 19.7 %copy-start.19 = (bf16[256,512]{1,0:T(8,128)(2,1)}, bf16[256,512]{1,0:T(8,128)(2,1)S(1)}, u32[]{:S(2)}) copy-start(bf16[256,512]{1,0:T(8,128)(2,1)S(1)} %collective-permute-done.2.refs_2_) | copy-start | bytes 786436
  93.2 7.3 %collective-permute-start.15 = (bf16[2,256,256]{2,1,0:T(8,128)(2,1)S(1)}, bf16[2,256,256]{2,1,0:T(8,128)(2,1)S(1)}, u32[]{:S(2)}, u32[]{:S(2)}) collective-permute-start(bf16[2,256,256]{2,1,0:T(8,128)(2,1)S(1)} %collective-permute-done.14.refs_10_), channel_id=1, source_target_pairs={{0,16},{16,0},{1,17},{17,1},{2,18},{18,2},{3,19},{19,3},{4,20},{20... | collective-permute-start | bytes 786440 | tf_op jit(solution)/shard_map/ppermute | solution.py:17
  93.7 16.2 %collective-permute-start.18 = (bf16[768,512]{1,0:T(8,128)(2,1)S(1)}, bf16[768,512]{1,0:T(8,128)(2,1)S(1)}, u32[]{:S(2)}, u32[]{:S(2)}) collective-permute-start(bf16[768,512]{1,0:T(8,128)(2,1)S(1)} %constant_dynamic-update-slice_fusion.refs_4_), channel_id=1, source_target_pairs={{0,1},{1,0},{2,3},{3,2},{4,5},{5,4},{6,7},{7,6},{8,9},{9,8},{10,11... | collective-permute-start | bytes 2359304 | tf_op jit(solution)/shard_map/ppermute | solution.py:26
  93.7 19.3 %copy-start.4 = (bf16[768,512]{1,0:T(8,128)(2,1)}, bf16[768,512]{1,0:T(8,128)(2,1)S(1)}, u32[]{:S(2)}) copy-start(bf16[768,512]{1,0:T(8,128)(2,1)S(1)} %collective-permute-done.19.refs_6_) | copy-start | bytes 2359300
  93.7 16.7 %collective-permute-start.20 = (bf16[768,512]{1,0:T(8,128)(2,1)S(1)}, bf16[768,512]{1,0:T(8,128)(2,1)S(1)}, u32[]{:S(2)}, u32[]{:S(2)}) collective-permute-start(bf16[768,512]{1,0:T(8,128)(2,1)S(1)} %collective-permute-done.19.refs_6_), channel_id=1, source_target_pairs={{0,1},{1,0},{2,3},{3,2},{4,5},{5,4},{6,7},{7,6},{8,9},{9,8},{10,11... | collective-permute-start | bytes 2359304 | tf_op jit(solution)/shard_map/ppermute | solution.py:26
  94.4 17.5 %collective-permute-start.8 = (bf16[768,512]{1,0:T(8,128)(2,1)S(1)}, bf16[768,512]{1,0:T(8,128)(2,1)S(1)}, u32[]{:S(2)}, u32[]{:S(2)}) collective-permute-start(bf16[768,512]{1,0:T(8,128)(2,1)S(1)} %collective-permute-done.7.refs_4_), channel_id=1, source_target_pairs={{0,1},{1,0},{2,3},{3,2},{4,5},{5,4},{6,7},{7,6},{8,9},{9,8},{10,11... | collective-permute-start | bytes 2359304 | tf_op jit(solution)/shard_map/ppermute | solution.py:26
  94.5 25.4 %copy-start.3 = (bf16[768,512]{1,0:T(8,128)(2,1)}, bf16[768,512]{1,0:T(8,128)(2,1)S(1)}, u32[]{:S(2)}) copy-start(bf16[768,512]{1,0:T(8,128)(2,1)S(1)} %collective-permute-done.9.refs_6_) | copy-start | bytes 2359300
  94.5 25.4 %collective-permute-start.10 = (bf16[768,512]{1,0:T(8,128)(2,1)S(1)}, bf16[768,512]{1,0:T(8,128)(2,1)}, u32[]{:S(2)}, u32[]{:S(2)}) collective-permute-start(bf16[768,512]{1,0:T(8,128)(2,1)S(1)} %collective-permute-done.9.refs_6_), channel_id=1, source_target_pairs={{0,1},{1,0},{2,3},{3,2},{4,5},{5,4},{6,7},{7,6},{8,9},{9,8},{10,11... | collective-permute-start | bytes 2359304 | tf_op jit(solution)/shard_map/ppermute | solution.py:26
  100.5 12.5 %copy-start.21 = (bf16[2,256,256]{2,1,0:T(8,128)(2,1)}, bf16[2,256,256]{2,1,0:T(8,128)(2,1)S(1)}, u32[]{:S(2)}) copy-start(bf16[2,256,256]{2,1,0:T(8,128)(2,1)S(1)} %collective-permute-done.15.refs_10_) | copy-start | bytes 786436
  100.5 6.4 %collective-permute-start.17 = (bf16[2,256,256]{2,1,0:T(8,128)(2,1)S(1)}, bf16[2,256,256]{2,1,0:T(8,128)(2,1)S(1)}, u32[]{:S(2)}, u32[]{:S(2)}) collective-permute-start(bf16[2,256,256]{2,1,0:T(8,128)(2,1)S(1)} %collective-permute-done.16.refs_11_), channel_id=1, source_target_pairs={{0,16},{16,0},{1,17},{17,1},{2,18},{18,2},{3,19},{19,3},{4,20},{20... | collective-permute-start | bytes 786440 | tf_op jit(solution)/shard_map/ppermute | solution.py:17
  106.9 6.0 %copy-start.22 = (bf16[2,256,256]{2,1,0:T(8,128)(2,1)}, bf16[2,256,256]{2,1,0:T(8,128)(2,1)S(1)}, u32[]{:S(2)}) copy-start(bf16[2,256,256]{2,1,0:T(8,128)(2,1)S(1)} %collective-permute-done.17.refs_11_) | copy-start | bytes 786436
  106.9 1.5 collective-permute-start.3
  108.4 4.5 %copy-start.23 = (bf16[256,512]{1,0:T(8,128)(2,1)}, bf16[256,512]{1,0:T(8,128)(2,1)S(1)}, u32[]{:S(2)}) copy-start(bf16[256,512]{1,0:T(8,128)(2,1)S(1)} %collective-permute-done.3.refs_3_) | copy-start | bytes 786436
  108.5 37.1 %collective-permute-start.29 = (bf16[256,512]{1,0:T(8,128)(2,1)}, bf16[256,512]{1,0:T(8,128)(2,1)}, u32[]{:S(2)}, u32[]{:S(2)}) collective-permute-start(bf16[256,512]{1,0:T(8,128)(2,1)} %collective-permute-done.27.refs_0_), channel_id=1, source_target_pairs={{0,2},{1,3},{2,0},{3,1},{4,6},{5,7},{6,4},{7,5},{8,10},{9,11},{10,... | collective-permute-start | bytes 786440 | tf_op jit(solution)/shard_map/ppermute | solution.py:26
  109.9 2.9 %copy-start.6 = (bf16[768,512]{1,0:T(8,128)(2,1)}, bf16[768,512]{1,0:T(8,128)(2,1)S(1)}, u32[]{:S(2)}) copy-start(bf16[768,512]{1,0:T(8,128)(2,1)S(1)} %collective-permute-done.18.refs_5_) | copy-start | bytes 2359300
  109.9 36.2 %collective-permute-start.33 = (bf16[256,512]{1,0:T(8,128)(2,1)}, bf16[256,512]{1,0:T(8,128)(2,1)}, u32[]{:S(2)}, u32[]{:S(2)}) collective-permute-start(bf16[256,512]{1,0:T(8,128)(2,1)} %collective-permute-done.31.refs_4_), channel_id=1, source_target_pairs={{0,2},{1,3},{2,0},{3,1},{4,6},{5,7},{6,4},{7,5},{8,10},{9,11},{10,... | collective-permute-start | bytes 786440 | tf_op jit(solution)/shard_map/ppermute | solution.py:26
  110.5 2.4 %copy-start.7 = (bf16[768,512]{1,0:T(8,128)(2,1)}, bf16[768,512]{1,0:T(8,128)(2,1)S(1)}, u32[]{:S(2)}) copy-start(bf16[768,512]{1,0:T(8,128)(2,1)S(1)} %collective-permute-done.20.refs_7_) | copy-start | bytes 2359300
  110.5 37.0 %collective-permute-start.37 = (bf16[256,512]{1,0:T(8,128)(2,1)}, bf16[256,512]{1,0:T(8,128)(2,1)}, u32[]{:S(2)}, u32[]{:S(2)}) collective-permute-start(bf16[256,512]{1,0:T(8,128)(2,1)} %collective-permute-done.35.refs_8_), channel_id=1, source_target_pairs={{0,2},{1,3},{2,0},{3,1},{4,6},{5,7},{6,4},{7,5},{8,10},{9,11},{10,... | collective-permute-start | bytes 786440 | tf_op jit(solution)/shard_map/ppermute | solution.py:26
  112.0 0.9 copy-start.5
  112.9 34.7 %collective-permute-start.28 = (bf16[256,512]{1,0:T(8,128)(2,1)}, bf16[256,512]{1,0:T(8,128)(2,1)}, u32[]{:S(2)}, u32[]{:S(2)}) collective-permute-start(bf16[256,512]{1,0:T(8,128)(2,1)} %collective-permute-done.27.refs_0_), channel_id=1, source_target_pairs={{0,1},{1,0},{2,3},{3,2},{4,5},{5,4},{6,7},{7,6},{8,9},{9,8},{10,11... | collective-permute-start | bytes 786440 | tf_op jit(solution)/shard_map/ppermute | solution.py:26
  128.2 8.0 %collective-permute-start.21 = (f32[8,128]{1,0:T(8,128)}, f32[8,128]{1,0:T(8,128)S(1)}, u32[]{:S(2)}, u32[]{:S(2)}) collective-permute-start(f32[8,128]{1,0:T(8,128)} %get-tuple-element.13), channel_id=1, source_target_pairs={{0,4},{4,8},{8,12},{12,0},{1,5},{5,9},{9,13},{13,1},{2,6},{6,10},{... | collective-permute-start | bytes 12296 | tf_op jit(solution)/shard_map/ppermute | solution.py:17
  136.3 4.7 %collective-permute-start.22 = (f32[8,128]{1,0:T(8,128)}, f32[8,128]{1,0:T(8,128)S(1)}, u32[]{:S(2)}, u32[]{:S(2)}) collective-permute-start(f32[8,128]{1,0:T(8,128)} %get-tuple-element.13), channel_id=1, source_target_pairs={{0,8},{4,12},{8,0},{12,4},{1,9},{5,13},{9,1},{13,5},{2,10},{6,14},... | collective-permute-start | bytes 12296 | tf_op jit(solution)/shard_map/ppermute | solution.py:17
  141.0 3.8 %collective-permute-start.23 = (f32[8,128]{1,0:T(8,128)}, f32[8,128]{1,0:T(8,128)S(1)}, u32[]{:S(2)}, u32[]{:S(2)}) collective-permute-start(f32[8,128]{1,0:T(8,128)} %get-tuple-element.13), channel_id=1, source_target_pairs={{0,12},{4,0},{8,4},{12,8},{1,13},{5,1},{9,5},{13,9},{2,14},{6,2},{... | collective-permute-start | bytes 12296 | tf_op jit(solution)/shard_map/ppermute | solution.py:17
  145.5 3.0 %collective-permute-start.24 = (f32[8,128]{1,0:T(8,128)S(1)}, f32[8,128]{1,0:T(8,128)S(1)}, u32[]{:S(2)}, u32[]{:S(2)}) collective-permute-start(f32[8,128]{1,0:T(8,128)S(1)} %add_add_fusion.1), channel_id=1, source_target_pairs={{0,1},{1,2},{2,3},{3,0},{4,5},{5,6},{6,7},{7,4},{8,9},{9,10},{10,1... | collective-permute-start | bytes 12296 | tf_op jit(solution)/shard_map/ppermute | solution.py:17
  145.5 3.7 %collective-permute-start.25 = (f32[8,128]{1,0:T(8,128)S(1)}, f32[8,128]{1,0:T(8,128)S(1)}, u32[]{:S(2)}, u32[]{:S(2)}) collective-permute-start(f32[8,128]{1,0:T(8,128)S(1)} %add_add_fusion.1), channel_id=1, source_target_pairs={{0,2},{1,3},{2,0},{3,1},{4,6},{5,7},{6,4},{7,5},{8,10},{9,11},{10,... | collective-permute-start | bytes 12296 | tf_op jit(solution)/shard_map/ppermute | solution.py:17
  146.1 3.1 %collective-permute-start.26 = (f32[8,128]{1,0:T(8,128)S(1)}, f32[8,128]{1,0:T(8,128)S(1)}, u32[]{:S(2)}, u32[]{:S(2)}) collective-permute-start(f32[8,128]{1,0:T(8,128)S(1)} %add_add_fusion.1), channel_id=1, source_target_pairs={{0,3},{1,0},{2,1},{3,2},{4,7},{5,4},{6,5},{7,6},{8,11},{9,8},{10,9... | collective-permute-start | bytes 12296 | tf_op jit(solution)/shard_map/ppermute | solution.py:17
  147.5 5.8 %collective-permute-start.32 = (bf16[256,512]{1,0:T(8,128)(2,1)}, bf16[256,512]{1,0:T(8,128)(2,1)S(1)}, u32[]{:S(2)}, u32[]{:S(2)}) collective-permute-start(bf16[256,512]{1,0:T(8,128)(2,1)} %collective-permute-done.31.refs_4_), channel_id=1, source_target_pairs={{0,1},{1,0},{2,3},{3,2},{4,5},{5,4},{6,7},{7,6},{8,9},{9,8},{10,11... | collective-permute-start | bytes 786440 | tf_op jit(solution)/shard_map/ppermute | solution.py:26
  147.5 5.8 %collective-permute-start.36 = (bf16[256,512]{1,0:T(8,128)(2,1)}, bf16[256,512]{1,0:T(8,128)(2,1)S(1)}, u32[]{:S(2)}, u32[]{:S(2)}) collective-permute-start(bf16[256,512]{1,0:T(8,128)(2,1)} %collective-permute-done.35.refs_8_), channel_id=1, source_target_pairs={{0,1},{1,0},{2,3},{3,2},{4,5},{5,4},{6,7},{7,6},{8,9},{9,8},{10,11... | collective-permute-start | bytes 786440 | tf_op jit(solution)/shard_map/ppermute | solution.py:26
  148.5 4.8 %collective-permute-start.30 = (bf16[256,512]{1,0:T(8,128)(2,1)}, bf16[256,512]{1,0:T(8,128)(2,1)S(1)}, u32[]{:S(2)}, u32[]{:S(2)}) collective-permute-start(bf16[256,512]{1,0:T(8,128)(2,1)} %collective-permute-done.29.refs_2_), channel_id=1, source_target_pairs={{0,1},{1,0},{2,3},{3,2},{4,5},{5,4},{6,7},{7,6},{8,9},{9,8},{10,11... | collective-permute-start | bytes 786440 | tf_op jit(solution)/shard_map/ppermute | solution.py:26
  149.2 4.2 %collective-permute-start.34 = (bf16[256,512]{1,0:T(8,128)(2,1)}, bf16[256,512]{1,0:T(8,128)(2,1)S(1)}, u32[]{:S(2)}, u32[]{:S(2)}) collective-permute-start(bf16[256,512]{1,0:T(8,128)(2,1)} %collective-permute-done.33.refs_6_), channel_id=1, source_target_pairs={{0,1},{1,0},{2,3},{3,2},{4,5},{5,4},{6,7},{7,6},{8,9},{9,8},{10,11... | collective-permute-start | bytes 786440 | tf_op jit(solution)/shard_map/ppermute | solution.py:26
  149.2 4.2 %collective-permute-start.38 = (bf16[256,512]{1,0:T(8,128)(2,1)}, bf16[256,512]{1,0:T(8,128)(2,1)S(1)}, u32[]{:S(2)}, u32[]{:S(2)}) collective-permute-start(bf16[256,512]{1,0:T(8,128)(2,1)} %collective-permute-done.37.refs_10_), channel_id=1, source_target_pairs={{0,1},{1,0},{2,3},{3,2},{4,5},{5,4},{6,7},{7,6},{8,9},{9,8},{10,11... | collective-permute-start | bytes 786440 | tf_op jit(solution)/shard_map/ppermute | solution.py:26
  153.3 0.8 copy-start.10
  153.3 0.8 copy-start.11
  153.4 0.9 copy-start.12
  153.4 1.0 copy-start.13
  170.5 18.4 %collective-permute-start.39 = (bf16[2,256,256]{2,1,0:T(8,128)(2,1)}, bf16[2,256,256]{2,1,0:T(8,128)(2,1)S(1)}, u32[]{:S(2)}, u32[]{:S(2)}) collective-permute-start(bf16[2,256,256]{2,1,0:T(8,128)(2,1)} %get-tuple-element.19), channel_id=1, source_target_pairs={{0,12},{4,0},{8,4},{12,8},{1,13},{5,1},{9,5},{13,9},{2,14},{6,2},{... | collective-permute-start | bytes 786440 | tf_op jit(solution)/shard_map/ppermute | solution.py:17
  174.3 20.7 %collective-permute-start.40 = (bf16[2,256,256]{2,1,0:T(8,128)(2,1)}, bf16[2,256,256]{2,1,0:T(8,128)(2,1)S(1)}, u32[]{:S(2)}, u32[]{:S(2)}) collective-permute-start(bf16[2,256,256]{2,1,0:T(8,128)(2,1)} %get-tuple-element.20), channel_id=1, source_target_pairs={{0,8},{4,12},{8,0},{12,4},{1,9},{5,13},{9,1},{13,5},{2,10},{6,14},... | collective-permute-start | bytes 786440 | tf_op jit(solution)/shard_map/ppermute | solution.py:17
  174.3 20.7 %copy-start.8 = (f32[2,256,256]{2,1,0:T(8,128)S(1)}, f32[2,256,256]{2,1,0:T(8,128)}, u32[]{:S(2)}) copy-start(f32[2,256,256]{2,1,0:T(8,128)} %get-tuple-element.18) | copy-start | bytes 1572868
  174.3 20.7 %collective-permute-start.41 = (bf16[2,256,256]{2,1,0:T(8,128)(2,1)}, bf16[2,256,256]{2,1,0:T(8,128)(2,1)S(1)}, u32[]{:S(2)}, u32[]{:S(2)}) collective-permute-start(bf16[2,256,256]{2,1,0:T(8,128)(2,1)} %get-tuple-element.21), channel_id=1, source_target_pairs={{0,4},{4,8},{8,12},{12,0},{1,5},{5,9},{9,13},{13,1},{2,6},{6,10},{... | collective-permute-start | bytes 786440 | tf_op jit(solution)/shard_map/ppermute | solution.py:17
  (2 other events, 1.4 us)
where the time goes:
time: 197 us; the launch traced here: 196 us
  waiting for transfers between devices  89.4 us (45%)
  starting transfers between devices  50.1 us (25%)
  Pallas kernels  45.2 us (23%)
  local copies, waits for them, and re-layouts  8.05 us (4%)
  other arithmetic  2.1 us (1%)
    ppermute x24, waiting for transfers between devices, shift(): return lax.ppermute(x, axis, [(i, (i + k) % n) for i in range(n)])  74.1 us
    ppermute x24, starting transfers between devices, shift(): return lax.ppermute(x, axis, [(i, (i + k) % n) for i in range(n)])  40.3 us
    pallas_call x1, Pallas kernels, per_device(): pl.pallas_call(functools.partial(project_kernel, n_f, n_t, n_f - 1, count...  16.1 us
    ppermute x18, waiting for transfers between devices, spread(): lax.ppermute(piece, axis, [(i, i ^ stride) for i in range(n)])  15.2 us
    pallas_call x1, Pallas kernels, per_device(): pl.pallas_call(functools.partial(update_kernel, count), grid=(2, shard //...  13.9 us
    ppermute x18, starting transfers between devices, spread(): lax.ppermute(piece, axis, [(i, i ^ stride) for i in range(n)])  9.76 us
    pallas_call x1, Pallas kernels, per_device(): pl.pallas_call(functools.partial(grad_kernel, n_f, n_t, False, 2), out_sh...  8.35 us
    pallas_call x1, Pallas kernels, per_device(): pl.pallas_call(functools.partial(grad_kernel, n_f, n_t, True, 2), out_sha...  6.86 us
  transfers between devices with their start and end apart: 42, of which 16 were waited for; matrix products, arithmetic and copies ran while one was open for 2% of the time, Pallas kernels for 15%

commit v1 on v0

v1 whole, which is shorter than its diff:
```python
import functools
from typing import NamedTuple

import jax
import jax.numpy as jnp
from jax import lax
from jax.experimental import pallas as pl
from jax.experimental.pallas import tpu as pltpu
from jax.sharding import PartitionSpec as P

STEP = 10
VMEM = pl.BlockSpec(memory_space=pltpu.VMEM)
HBM = pl.BlockSpec(memory_space=pl.ANY)
SMEM = pl.BlockSpec(memory_space=pltpu.SMEM)
PARAMS = pltpu.CompilerParams(vmem_limit_bytes=12 * 2**20)


class Plan(NamedTuple):
    sources: int
    n_t: int
    outs: tuple


def near(x):
    return pltpu.with_memory_space_constraint(x, pltpu.VMEM)


def far(x):
    return pltpu.with_memory_space_constraint(x, pltpu.HBM)


def shift(x, axis, k):
    n = lax.axis_size(axis)
    return lax.ppermute(x, axis, [(i, (i + k) % n) for i in range(n)])


def trade(x, axis, k):
    n = lax.axis_size(axis)
    return lax.ppermute(x, axis, [(i, i ^ k) for i in range(n)])


def spread(pieces, axis):
    n = lax.axis_size(axis)
    held = {0: list(pieces)}
    stride = n // 2
    while stride:
        for r, group in list(held.items()):
            if stride == 1 and len(group) > 1:
                group = [jnp.concatenate(group, axis=0)]
            moved = []
            for piece in group:
                moved.append(lax.ppermute(piece, axis, [(j, j ^ stride) for j in range(n)]))
            held[r ^ stride] = moved
        stride //= 2
    return [held[r] for r in range(n)]


def contract_rows(a, b):
    return lax.dot_general(a, b, (((0,), (0,)), ((), ())), preferred_element_type=jnp.float32)


def row_blocks(refs, rows):
    return [ref[i : i + rows, :] for ref in refs for i in range(0, ref.shape[0], rows)]


def split(refs, sizes):
    groups = []
    for size in sizes:
        groups.append(refs[:size])
        refs = refs[size:]
    return groups, refs


def grad_kernel(sizes, n_f, own, at_ref, *refs):
    tokens, refs = split(refs, sizes)
    cots, refs = refs[:n_f], refs[n_f:]
    rows, chunk = cots[0].shape[1], tokens[0][0].shape[1]
    squares = jnp.zeros((8, 128), jnp.float32)
    for r, group in enumerate(tokens):
        at = pl.multiple_of((at_ref[0] ^ r) * chunk, chunk)
        for s in range(2):
            blocks = row_blocks(group, rows)
            acc = functools.reduce(jnp.add, [contract_rows(b, c[s]) for b, c in zip(blocks, cots, strict=True)])
            if own:
                refs[0][s, pl.ds(at, chunk), :] = acc
            else:
                acc += refs[0][s, pl.ds(at, chunk), :]
                refs[1][s, pl.ds(at, chunk), :] = acc
                squares += jnp.sum((acc * acc).reshape(-1, 8, 128), axis=0)
    if not own:
        refs[2][...] = squares


def clip_scale(squares, count):
    total = jnp.sum(squares)
    return jnp.minimum(1.0, 1.0 / jnp.sqrt(jnp.full((8, 128), total / count, jnp.float32) + 1e-06))[:1, :1]


def adam_update(scale, grad, master, first_moment, second_moment):
    clipped = scale * grad
    new_first = 0.9 * first_moment + 0.1 * clipped
    new_second = 0.95 * second_moment + (0.05 * clipped) * clipped
    second_hat = new_second * (1.0 / (1.0 - 0.95**STEP))
    root = second_hat * lax.rsqrt(second_hat)
    step = (0.003 / (1.0 - 0.9**STEP)) * new_first / (root + 1e-08)
    new_master = (1.0 - 0.003 * 0.1) * master - step
    return (new_master, new_first, new_second)


def project_kernel(sizes, rows, n_f, count, at_ref, squares_ref, grad_ref, master_ref, m_ref, v_ref, *refs):
    tokens, refs = split(refs, sizes)
    outs, weight = refs[:n_f], refs[n_f]
    chunk, shard = tokens[0][0].shape[1], weight.shape[1]
    block = min(shard, 128)
    scale = clip_scale(squares_ref[...], count)
    for s in range(2):

        def update_block(b, carry, s=s):
            part = pl.ds(pl.multiple_of(b * block, block), block)
            at = (s, part, slice(None))
            new_master, _, _ = adam_update(scale, grad_ref[at], master_ref[at], m_ref[at], v_ref[at])
            weight[at] = new_master.astype(jnp.bfloat16)
            return carry

        lax.fori_loop(0, shard // block, update_block, 0)
        blocks = [row_blocks(group, rows) for group in tokens]
        for k in range(n_f):
            acc = jnp.zeros(outs[0].shape[1:], jnp.float32)
            for r, group in enumerate(blocks):
                at = pl.multiple_of((at_ref[0] ^ r) * chunk, chunk)
                acc += jnp.dot(group[k], weight[s, pl.ds(at, chunk), :], preferred_element_type=jnp.float32)
            outs[k][s] = acc.astype(outs[k].dtype)


def stage_kernel(plan, at_ref, *refs):
    sources, outs, sems = refs[: plan.sources], refs[plan.sources : -1], refs[-1]
    copies = []
    for out, (source, block) in zip(outs, plan.outs, strict=True):
        ref = sources[source]
        if block is not None:
            chunk = out.shape[1]
            owner, r = block
            column = ((at_ref[1] ^ owner) * plan.n_t + (at_ref[0] ^ r)) * chunk
            ref = ref.at[:, pl.ds(pl.multiple_of(column, chunk), chunk)]
        copies.append(pltpu.make_async_copy(ref, out, sems.at[len(copies)]))
        copies[-1].start()
    for copy in copies:
        copy.wait()


def update_kernel(count, squares_ref, grad_ref, master_ref, m_ref, v_ref, *refs):
    outs, held, sems = refs[:3], refs[3:6], refs[6]
    shard = grad_ref.shape[1]
    block = min(shard, 128)
    span = min(shard, 512)
    scale = clip_scale(squares_ref[...], count)
    copies = []
    for s in range(2):
        for first in range(0, shard, span):

            def update_block(b, carry, s=s, first=first):
                at = (s, pl.ds(pl.multiple_of(first + b * block, block), block), slice(None))
                new = adam_update(scale, grad_ref[at], master_ref[at], m_ref[at], v_ref[at])
                for ref, value in zip(held, new, strict=True):
                    ref[at] = value
                return carry

            lax.fori_loop(0, span // block, update_block, 0)
            at = (s, pl.ds(first, span))
            for i in range(3):
                copies.append(pltpu.make_async_copy(held[i].at[at], outs[i].at[at], sems.at[len(copies)]))
                copies[-1].start()
    for copy in copies:
        copy.wait()


def per_device(tokens, next_tokens, cotangent, master, first_moment, second_moment):
    n_f, n_t = lax.axis_size("fsdp"), lax.axis_size("tensor")
    f, t = lax.axis_index("fsdp"), lax.axis_index("tensor")
    rows, width = tokens.shape
    shard = width // n_f
    chunk = shard // n_t
    kv = cotangent.shape[2]
    count = 2.0 * width * kv * n_t
    at = jnp.stack([t, f]).astype(jnp.int32)
    shard_shape = (2, shard, kv)

    def mine(x, owner, r=0):
        return lax.dynamic_slice(x, (0, (f ^ owner) * shard + (t ^ r) * chunk), (rows, chunk))

    def fetch(pieces):
        return [trade(piece, "fsdp", k) for k, piece in enumerate(pieces, 1)]

    state = (master, first_moment, second_moment)
    blocks = [(3, (0, r)) for r in range(n_t)] + [(4, (0, r)) for r in range(n_t)]
    blocks += [(4, (k, 0)) for k in range(1, n_f)]
    by_copy = chunk % 128 == 0
    outs = [(i, None) for i in range(3)] + (blocks if by_copy else [])
    staged = pl.pallas_call(
        functools.partial(stage_kernel, Plan(5, n_t, tuple(outs))),
        out_shape=(pltpu.VMEM(shard_shape, jnp.float32),) * 3
        + (pltpu.VMEM((rows, chunk), jnp.bfloat16),) * (len(outs) - 3),
        in_specs=[SMEM] + [HBM] * 5,
        out_specs=(VMEM,) * len(outs),
        scratch_shapes=[pltpu.SemaphoreType.DMA((len(outs),))],
        compiler_params=pltpu.CompilerParams(vmem_limit_bytes=2**20),
    )(at, *map(far, state), far(tokens), far(next_tokens))
    state, staged = staged[:3], staged[3:]
    if not by_copy:
        staged = [mine((tokens, next_tokens)[source - 3], owner, r) for source, (owner, r) in blocks]
    first, next_first, next_others = staged[:n_t], staged[n_t : 2 * n_t], staged[2 * n_t :]

    rest = fetch([mine(tokens, k) for k in range(1, n_f)])
    other = [shift(x, "dp", 1) for x in [mine(tokens, 0)] + rest]
    other = spread(other, "tensor")
    rest = spread(rest, "tensor")
    cots = [cotangent]
    for k in range(1, n_f):
        bit = k & -k
        cots.append(trade(cots[k ^ bit], "fsdp", bit))
    other_cots = [shift(c, "dp", 1) for c in cots]
    next_rest = spread(fetch(next_others), "tensor")

    def flat(groups):
        return [near(piece) for group in groups for piece in group], [len(group) for group in groups]

    tokens_in, sizes = flat([[a] + b for a, b in zip(first, rest, strict=True)])
    grad = pl.pallas_call(
        functools.partial(grad_kernel, sizes, n_f, True),
        out_shape=pltpu.VMEM(shard_shape, jnp.float32),
        in_specs=[SMEM] + [VMEM] * (len(tokens_in) + n_f),
        out_specs=VMEM,
        compiler_params=PARAMS,
    )(at, *tokens_in, *map(near, cots))
    tokens_in, sizes = flat(other)
    grad, squares = pl.pallas_call(
        functools.partial(grad_kernel, sizes, n_f, False),
        out_shape=(pltpu.VMEM(shard_shape, jnp.float32), jax.ShapeDtypeStruct((8, 128), jnp.float32)),
        in_specs=[SMEM] + [VMEM] * (len(tokens_in) + n_f + 1),
        out_specs=(VMEM, VMEM),
        compiler_params=PARAMS,
    )(at, *tokens_in, *map(near, other_cots), grad)

    for axis, n in (("fsdp", n_f), ("tensor", n_t)):
        squares = functools.reduce(jnp.add, [shift(squares, axis, k) for k in range(1, n)], squares)

    out = (2, rows, kv)
    tokens_in, sizes = flat([[a] + b for a, b in zip(next_first, next_rest, strict=True)])
    partial = pl.pallas_call(
        functools.partial(project_kernel, sizes, rows, n_f, count),
        out_shape=(jax.ShapeDtypeStruct(out, jnp.float32),)
        + (jax.ShapeDtypeStruct(out, jnp.bfloat16),) * (n_f - 1),
        in_specs=[SMEM] + [VMEM] * (5 + len(tokens_in)),
        out_specs=(VMEM,) * n_f,
        scratch_shapes=[pltpu.VMEM((2, shard, kv), jnp.bfloat16)],
        compiler_params=PARAMS,
    )(at, squares, grad, *state, *tokens_in)
    got = [trade(partial[k], "fsdp", k) for k in range(1, n_f)]
    projected = functools.reduce(jnp.add, [g.astype(jnp.float32) for g in got], partial[0])
    copies = 3 * 2 * (shard // min(shard, 512))
    new_master, new_first, new_second = pl.pallas_call(
        functools.partial(update_kernel, count),
        out_shape=(jax.ShapeDtypeStruct(shard_shape, jnp.float32),) * 3,
        in_specs=[VMEM] * 5,
        out_specs=(HBM,) * 3,
        scratch_shapes=[pltpu.VMEM(shard_shape, jnp.float32)] * 3 + [pltpu.SemaphoreType.DMA((copies,))],
        compiler_params=pltpu.CompilerParams(vmem_limit_bytes=16 * 2**20),
    )(squares, grad, *state)
    return (new_master, new_first, new_second, projected.astype(jnp.bfloat16))


def solution(mesh):
    in_specs = (
        P(("dp", "fsdp"), None),
        P(("dp", "fsdp"), None),
        P(None, ("dp", "fsdp"), "tensor"),
        P(None, "fsdp", "tensor"),
        P(None, "fsdp", "tensor"),
        P(None, "fsdp", "tensor"),
    )
    out_specs = (
        P(None, "fsdp", "tensor"),
        P(None, "fsdp", "tensor"),
        P(None, "fsdp", "tensor"),
        P(None, ("dp", "fsdp"), "tensor"),
    )
    return jax.shard_map(per_device, mesh=mesh, in_specs=in_specs, out_specs=out_specs, check_vma=False)
```

time: 197 us -> 177 us (0.90)
  Pallas kernels: 45.2 us -> 23.4 us
  starting transfers between devices: 50.1 us -> 62.9 us
  local copies, waits for them, and re-layouts: 8.05 us -> 1.31 us
  waiting for transfers between devices: 89.4 us -> 84.5 us
    ppermute x24 -> x14, waiting for transfers between devices: 74.1 us -> 16 us  [shift(): return lax.ppermute(x, axis, [(i, (i + k) % n) for i in range(n)])]
    ppermute x18 -> x28, waiting for transfers between devices: 15.2 us -> 68.5 us  [the longest x12 43.2 us: trade(): return lax.ppermute(x, axis, [(i, i ^ k) for i in range(n)])]
    ppermute x18 -> x28, starting transfers between devices: 9.76 us -> 38.4 us  [the longest x12 24.3 us: trade(): return lax.ppermute(x, axis, [(i, i ^ k) for i in range(n)])]
    pallas_call x4 -> x5, Pallas kernels: 45.2 us -> 23.4 us  [the longest x1 6.05 us: per_device(): pl.pallas_call(functools.partial(project_kernel, sizes, rows, n_f, count)...]
    ppermute x24 -> x14, starting transfers between devices: 40.3 us -> 24.4 us  [shift(): return lax.ppermute(x, axis, [(i, (i + k) % n) for i in range(n)])]
    dynamic_slice x3 -> x1, local copies, waits for them, and re-layouts: 5.86 us -> 1.31 us  [mine(): lax.dynamic_slice(x, (0, (f ^ owner) * shard + (t ^ r) * chunk), (rows, c...]
    unnamed x50 -> x2, local copies, waits for them, and re-layouts: 2.17 us -> 0.01 us
  transfers between devices with their start and end apart: 42 -> 42, of which waited for: 16 -> 22; matrix products, arithmetic and copies ran while one was open for 2% -> 0% of each run, Pallas kernels for 15% -> 10%
where the time goes in v1:
time: 177 us; the launch traced here: 174 us
  waiting for transfers between devices  84.5 us (48%)
  starting transfers between devices  62.9 us (36%)
  Pallas kernels  23.4 us (13%)
    ppermute x12, waiting for transfers between devices, trade(): return lax.ppermute(x, axis, [(i, i ^ k) for i in range(n)])  43.2 us
    ppermute x16, waiting for transfers between devices, spread(): moved.append(lax.ppermute(piece, axis, [(j, j ^ stride) for j in range(n)]))  25.3 us
    ppermute x14, starting transfers between devices, shift(): return lax.ppermute(x, axis, [(i, (i + k) % n) for i in range(n)])  24.4 us
    ppermute x12, starting transfers between devices, trade(): return lax.ppermute(x, axis, [(i, i ^ k) for i in range(n)])  24.3 us
    ppermute x14, waiting for transfers between devices, shift(): return lax.ppermute(x, axis, [(i, (i + k) % n) for i in range(n)])  16 us
    ppermute x16, starting transfers between devices, spread(): moved.append(lax.ppermute(piece, axis, [(j, j ^ stride) for j in range(n)]))  14.1 us
    pallas_call x1, Pallas kernels, per_device(): pl.pallas_call(functools.partial(project_kernel, sizes, rows, n_f, count)...  6.05 us
    pallas_call x1, Pallas kernels, per_device(): pl.pallas_call(functools.partial(stage_kernel, Plan(5, n_t, tuple(outs)))...  6.03 us
  transfers between devices with their start and end apart: 42, of which 22 were waited for; matrix products, arithmetic and copies ran while one was open for 0% of the time, Pallas kernels for 10%

profile of v1, /device:TPU:0, one launch (start us, length us, event | category | flops | bytes accessed | tf_op | source)
XLA Modules:
  0.0 174.2 jit_solution(17096919005677452101)
XLA Ops:
  0.7 1.3 constant_dynamic-slice_fusion
  2.0 3.1 %collective-permute-start.1 = (bf16[256,512]{1,0:T(8,128)(2,1)S(1)}, bf16[256,512]{1,0:T(8,128)(2,1)S(1)}, u32[]{:S(2)}, u32[]{:S(2)}) collective-permute-start(bf16[256,512]{1,0:T(8,128)(2,1)S(1)} %get-tuple-element.52), channel_id=1, source_target_pairs={{0,4},{4,0},{8,12},{12,8},{1,5},{5,1},{9,13},{13,9},{2,6},{6,2},{1... | collective-permute-start | bytes 786440 | tf_op jit(solution)/shard_map/ppermute | solution.py:39
  5.1 2.6 %collective-permute-start.3 = (bf16[256,512]{1,0:T(8,128)(2,1)S(1)}, bf16[256,512]{1,0:T(8,128)(2,1)S(1)}, u32[]{:S(2)}, u32[]{:S(2)}) collective-permute-start(bf16[256,512]{1,0:T(8,128)(2,1)S(1)} %get-tuple-element.51), channel_id=1, source_target_pairs={{0,8},{4,12},{8,0},{12,4},{1,9},{5,13},{9,1},{13,5},{2,10},{6,14},... | collective-permute-start | bytes 786440 | tf_op jit(solution)/shard_map/ppermute | solution.py:39
  7.7 1.9 %collective-permute-start.16 = (bf16[2,256,256]{2,1,0:T(8,128)(2,1)S(1)}, bf16[2,256,256]{2,1,0:T(8,128)(2,1)S(1)}, u32[]{:S(2)}, u32[]{:S(2)}) collective-permute-start(bf16[2,256,256]{2,1,0:T(8,128)(2,1)S(1)} %copy-done), channel_id=1, source_target_pairs={{0,8},{4,12},{8,0},{12,4},{1,9},{5,13},{9,1},{13,5},{2,10},{6,14},... | collective-permute-start | bytes 786440 | tf_op jit(solution)/shard_map/ppermute | solution.py:39
  9.6 2.5 %collective-permute-start.14 = (bf16[2,256,256]{2,1,0:T(8,128)(2,1)S(1)}, bf16[2,256,256]{2,1,0:T(8,128)(2,1)S(1)}, u32[]{:S(2)}, u32[]{:S(2)}) collective-permute-start(bf16[2,256,256]{2,1,0:T(8,128)(2,1)S(1)} %copy-done), channel_id=1, source_target_pairs={{0,4},{4,0},{8,12},{12,8},{1,5},{5,1},{9,13},{13,9},{2,6},{6,2},{1... | collective-permute-start | bytes 786440 | tf_op jit(solution)/shard_map/ppermute | solution.py:39
  12.1 0.1 pad_add_fusion.at_ref
  12.1 6.0 %shard_map.93 = (f32[2,2048,256]{2,1,0:T(8,128)S(1)}, f32[2,2048,256]{2,1,0:T(8,128)S(1)}, f32[2,2048,256]{2,1,0:T(8,128)S(1)}, bf16[256,512]{1,0:T(8,128)(2,1)S...) custom-call(s32[2]{0:T(128)S(1)} %pad_add_fusion.at_ref, ...), custom_call_target="tpu_custom_call" | custom-call | tf_op jit(solution)/shard_map/pallas_call | solution.py:199
  18.2 1.6 collective-permute-start
  19.8 12.3 %collective-permute-done.3.refs_2_ = bf16[256,512]{1,0:T(8,128)(2,1)S(1)} collective-permute-done((bf16[256,512]{1,0:T(8,128)(2,1)S(1)}, bf16[256,512]{1,0:T(8,128)(2,1)S(1)}, u32[]{:S(2)}, u32[]{:S(2)}) %collective-permute-start.3) | collective-permute-done | bytes 262176 | tf_op jit(solution)/shard_map/ppermute | solution.py:39
  32.1 1.5 collective-permute-start.13
  33.6 4.7 %collective-permute-start.31 = (bf16[256,512]{1,0:T(8,128)(2,1)S(1)}, bf16[256,512]{1,0:T(8,128)(2,1)S(1)}, u32[]{:S(2)}, u32[]{:S(2)}) collective-permute-start(bf16[256,512]{1,0:T(8,128)(2,1)S(1)} %get-tuple-element.40), channel_id=1, source_target_pairs={{0,4},{4,0},{8,12},{12,8},{1,5},{5,1},{9,13},{13,9},{2,6},{6,2},{1... | collective-permute-start | bytes 786440 | tf_op jit(solution)/shard_map/ppermute | solution.py:39
  38.2 3.8 %collective-permute-done.16.refs_14_ = bf16[2,256,256]{2,1,0:T(8,128)(2,1)S(1)} collective-permute-done((bf16[2,256,256]{2,1,0:T(8,128)(2,1)S(1)}, bf16[2,256,256]{2,1,0:T(8,128)(2,1)S(1)}, u32[]{:S(2)}, u32[]{:S(2)}) %collective-permute-start.16) | collective-permute-done | bytes 262176 | tf_op jit(solution)/shard_map/ppermute | solution.py:39
  42.0 2.5 %collective-permute-start.33 = (bf16[256,512]{1,0:T(8,128)(2,1)S(1)}, bf16[256,512]{1,0:T(8,128)(2,1)S(1)}, u32[]{:S(2)}, u32[]{:S(2)}) collective-permute-start(bf16[256,512]{1,0:T(8,128)(2,1)S(1)} %get-tuple-element.42), channel_id=1, source_target_pairs={{0,12},{4,8},{8,4},{12,0},{1,13},{5,9},{9,5},{13,1},{2,14},{6,10},... | collective-permute-start | bytes 786440 | tf_op jit(solution)/shard_map/ppermute | solution.py:39
  44.5 1.5 collective-permute-start.21
  46.0 0.5 collective-permute-start.22
  46.6 1.4 collective-permute-done.31.refs_1_
  48.0 1.5 collective-permute-start.4
  49.5 12.5 %collective-permute-done.32.refs_2_ = bf16[256,512]{1,0:T(8,128)(2,1)S(1)} collective-permute-done((bf16[256,512]{1,0:T(8,128)(2,1)S(1)}, bf16[256,512]{1,0:T(8,128)(2,1)S(1)}, u32[]{:S(2)}, u32[]{:S(2)}) %collective-permute-start.32) | collective-permute-done | bytes 262176 | tf_op jit(solution)/shard_map/ppermute | solution.py:39
  62.0 1.5 collective-permute-start.6
  63.5 0.5 collective-permute-start.2
  64.0 1.5 collective-permute-start.23
  65.5 0.5 collective-permute-start.8
  66.1 1.5 collective-permute-start.10
  67.6 3.5 %collective-permute-done.6.refs_3_ = bf16[256,512]{1,0:T(8,128)(2,1)S(1)} collective-permute-done((bf16[256,512]{1,0:T(8,128)(2,1)S(1)}, bf16[256,512]{1,0:T(8,128)(2,1)S(1)}, u32[]{:S(2)}, u32[]{:S(2)}) %collective-permute-start.6) | collective-permute-done | bytes 262176 | tf_op jit(solution)/shard_map/ppermute | solution.py:34
  71.1 1.5 collective-permute-start.11
  72.6 1.3 collective-permute-done.2.refs_1_
  73.9 1.5 collective-permute-start.9
  75.5 2.4 %collective-permute-start.18 = (bf16[2,256,256]{2,1,0:T(8,128)(2,1)S(1)}, bf16[2,256,256]{2,1,0:T(8,128)(2,1)S(1)}, u32[]{:S(2)}, u32[]{:S(2)}) collective-permute-start(bf16[2,256,256]{2,1,0:T(8,128)(2,1)S(1)} %collective-permute-done.16.refs_14_), channel_id=1, source_target_pairs={{0,4},{4,0},{8,12},{12,8},{1,5},{5,1},{9,13},{13,9},{2,6},{6,2},{1... | collective-permute-start | bytes 786440 | tf_op jit(solution)/shard_map/ppermute | solution.py:39
  77.9 1.0 collective-permute-done.8.refs_5_
  78.8 1.5 collective-permute-start.17
  80.4 4.1 %collective-permute-done.10.refs_7_ = bf16[256,512]{1,0:T(8,128)(2,1)S(1)} collective-permute-done((bf16[256,512]{1,0:T(8,128)(2,1)S(1)}, bf16[256,512]{1,0:T(8,128)(2,1)S(1)}, u32[]{:S(2)}, u32[]{:S(2)}) %collective-permute-start.10) | collective-permute-done | bytes 262176 | tf_op jit(solution)/shard_map/ppermute | solution.py:52
  84.5 1.5 collective-permute-start.35
  86.0 4.1 %collective-permute-done.11.refs_8_ = bf16[256,512]{1,0:T(8,128)(2,1)S(1)} collective-permute-done((bf16[256,512]{1,0:T(8,128)(2,1)S(1)}, bf16[256,512]{1,0:T(8,128)(2,1)S(1)}, u32[]{:S(2)}, u32[]{:S(2)}) %collective-permute-start.11) | collective-permute-done | bytes 262176 | tf_op jit(solution)/shard_map/ppermute | solution.py:52
  90.1 5.6 %collective-permute-done.9.refs_6_ = bf16[256,512]{1,0:T(8,128)(2,1)S(1)} collective-permute-done((bf16[256,512]{1,0:T(8,128)(2,1)S(1)}, bf16[256,512]{1,0:T(8,128)(2,1)S(1)}, u32[]{:S(2)}, u32[]{:S(2)}) %collective-permute-start.9) | collective-permute-done | bytes 262176 | tf_op jit(solution)/shard_map/ppermute | solution.py:52
  95.7 1.5 collective-permute-start.36
  97.4 0.5 collective-permute-start.7
  97.9 2.8 %collective-permute-done.35.refs_7_ = bf16[256,512]{1,0:T(8,128)(2,1)S(1)} collective-permute-done((bf16[256,512]{1,0:T(8,128)(2,1)S(1)}, bf16[256,512]{1,0:T(8,128)(2,1)S(1)}, u32[]{:S(2)}, u32[]{:S(2)}) %collective-permute-start.35) | collective-permute-done | bytes 262176 | tf_op jit(solution)/shard_map/ppermute | solution.py:52
  100.7 2.8 %collective-permute-done.36.refs_8_ = bf16[256,512]{1,0:T(8,128)(2,1)S(1)} collective-permute-done((bf16[256,512]{1,0:T(8,128)(2,1)S(1)}, bf16[256,512]{1,0:T(8,128)(2,1)S(1)}, u32[]{:S(2)}, u32[]{:S(2)}) %collective-permute-start.36) | collective-permute-done | bytes 262176 | tf_op jit(solution)/shard_map/ppermute | solution.py:52
  103.5 1.5 collective-permute-start.37
  105.0 4.9 %collective-permute-done.37.refs_9_ = bf16[256,512]{1,0:T(8,128)(2,1)S(1)} collective-permute-done((bf16[256,512]{1,0:T(8,128)(2,1)S(1)}, bf16[256,512]{1,0:T(8,128)(2,1)S(1)}, u32[]{:S(2)}, u32[]{:S(2)}) %collective-permute-start.37) | collective-permute-done | bytes 262176 | tf_op jit(solution)/shard_map/ppermute | solution.py:52
  109.8 1.5 collective-permute-start.15
  111.5 4.7 %collective-permute-done.15.refs_11_ = bf16[2,256,256]{2,1,0:T(8,128)(2,1)S(1)} collective-permute-done((bf16[2,256,256]{2,1,0:T(8,128)(2,1)S(1)}, bf16[2,256,256]{2,1,0:T(8,128)(2,1)S(1)}, u32[]{:S(2)}, u32[]{:S(2)}) %collective-permute-start.15) | collective-permute-done | bytes 262176 | tf_op jit(solution)/shard_map/ppermute | solution.py:34
  116.2 0.5 collective-permute-start.38
  116.7 1.5 collective-permute-start.19
  118.2 2.9 %shard_map.94.refs_14_ = f32[2,2048,256]{2,1,0:T(8,128)S(1)} custom-call(s32[2]{0:T(128)S(1)} %pad_add_fusion.at_ref, bf16[256,512]{1,0:T(8,128)(2,1)S(1)} %get-tuple-element.27.refs_0_, bf16[256,512]{1,0:T(8,128)(2,1)S(1)} %collective-permute-done.1.refs_1_, bf16[256,512]{1,0:T(8,128)(2,1)S(1)} %collective-permute-done.3.refs_2_, ...), custom_call_target="tpu_custom_call" | custom-call | tf_op jit(solution)/shard_map/pallas_call | solution.py:228
  121.2 3.8 %collective-permute-done.19.refs_13_ = bf16[2,256,256]{2,1,0:T(8,128)(2,1)S(1)} collective-permute-done((bf16[2,256,256]{2,1,0:T(8,128)(2,1)S(1)}, bf16[2,256,256]{2,1,0:T(8,128)(2,1)S(1)}, u32[]{:S(2)}, u32[]{:S(2)}) %collective-permute-start.19) | collective-permute-done | bytes 262176 | tf_op jit(solution)/shard_map/ppermute | solution.py:34
  125.0 3.2 %shard_map.95 = (f32[2,2048,256]{2,1,0:T(8,128)S(1)}, f32[8,128]{1,0:T(8,128)S(1)}) custom-call(s32[2]{0:T(128)S(1)} %pad_add_fusion.at_ref, bf16[256,512]{1,0:T(8,128)(2,1)S(1)} %collective-permute-done.refs_0_, bf16[256,512]{1,0:T(8,128)(2,1)S(1)} %collective-permute-done.2.refs_1_, bf16[256,512]{1,0:T(8,128)(2,1)S(1)} %collective-permute-done.4.refs_2_, ...), custom_call_target="tpu_custom_call" | custom-call | tf_op jit(solution)/shard_map/pallas_call | solution.py:236
  128.2 6.0 %collective-permute-start.25 = (f32[8,128]{1,0:T(8,128)S(1)}, f32[8,128]{1,0:T(8,128)S(1)}, u32[]{:S(2)}, u32[]{:S(2)}) collective-permute-start(f32[8,128]{1,0:T(8,128)S(1)} %get-tuple-element.31), channel_id=1, source_target_pairs={{0,4},{4,8},{8,12},{12,0},{1,5},{5,9},{9,13},{13,1},{2,6},{6,10},{... | collective-permute-start | bytes 12296 | tf_op jit(solution)/shard_map/ppermute | solution.py:34
  134.2 1.4 collective-permute-start.26
  135.6 2.8 %collective-permute-start.27 = (f32[8,128]{1,0:T(8,128)S(1)}, f32[8,128]{1,0:T(8,128)S(1)}, u32[]{:S(2)}, u32[]{:S(2)}) collective-permute-start(f32[8,128]{1,0:T(8,128)S(1)} %get-tuple-element.31), channel_id=1, source_target_pairs={{0,12},{4,0},{8,4},{12,8},{1,13},{5,1},{9,5},{13,9},{2,14},{6,2},{... | collective-permute-start | bytes 12296 | tf_op jit(solution)/shard_map/ppermute | solution.py:34
  138.5 0.2 collective-permute-done.26
  138.7 1.1 collective-permute-done.27
  139.8 1.5 collective-permute-start.29
  141.3 1.5 collective-permute-start.30
  142.8 0.1 collective-permute-done.28
  142.9 0.6 collective-permute-done.29
  143.4 0.7 collective-permute-done.30
  144.1 6.0 %shard_map.97 = (f32[2,256,256]{2,1,0:T(8,128)S(1)}, bf16[2,256,256]{2,1,0:T(8,128)(2,1)S(1)}, bf16[2,256,256]{2,1,0:T(8,128)(2,1)S(1)}, bf16[2,256,256]{2,1,0:T(8,128)(2,1)S(1)}) custom-call(s32[2]{0:T(128)S(1)} %pad_add_fusion.at_ref, f32[8,128]{1,0:T(8,128)S(1)} %add_add_fusion.squares_ref, f32[2,2048,256]{2,1,0:T(8,128)S(1)} %get-tuple-element.32.grad_ref, ...), custom_call_target="tpu_custom_call" | custom-call | tf_op jit(solution)/shard_map/pallas_call | solution.py:249
  150.2 0.9 collective-permute-start.39
  151.1 3.8 %collective-permute-start.40 = (bf16[2,256,256]{2,1,0:T(8,128)(2,1)S(1)}, bf16[2,256,256]{2,1,0:T(8,128)(2,1)S(1)}, u32[]{:S(2)}, u32[]{:S(2)}) collective-permute-start(bf16[2,256,256]{2,1,0:T(8,128)(2,1)S(1)} %get-tuple-element.48), channel_id=1, source_target_pairs={{0,8},{4,12},{8,0},{12,4},{1,9},{5,13},{9,1},{13,5},{2,10},{6,14},... | collective-permute-start | bytes 786440 | tf_op jit(solution)/shard_map/ppermute | solution.py:39
  154.9 5.2 %shard_map.96 = (f32[2,2048,256]{2,1,0:T(8,128)}, f32[2,2048,256]{2,1,0:T(8,128)}, f32[2,2048,256]{2,1,0:T(8,128)}) custom-call(f32[8,128]{1,0:T(8,128)S(1)} %add_add_fusion.squares_ref, f32[2,2048,256]{2,1,0:T(8,128)S(1)} %get-tuple-element.32.grad_ref, f32[2,2048,256]{2,1,0:T(8,128)S(1)} %get-tuple-element.33.master_ref, ...), custom_call_target="tpu_custom_call" | custom-call | tf_op jit(solution)/shard_map/pallas_call | solution.py:261
  160.1 4.3 %collective-permute-done.39 = bf16[2,256,256]{2,1,0:T(8,128)(2,1)S(1)} collective-permute-done((bf16[2,256,256]{2,1,0:T(8,128)(2,1)S(1)}, bf16[2,256,256]{2,1,0:T(8,128)(2,1)S(1)}, u32[]{:S(2)}, u32[]{:S(2)}) %collective-permute-start.39) | collective-permute-done | bytes 262176 | tf_op jit(solution)/shard_map/ppermute | solution.py:39
  164.4 8.9 %collective-permute-done.40 = bf16[2,256,256]{2,1,0:T(8,128)(2,1)S(1)} collective-permute-done((bf16[2,256,256]{2,1,0:T(8,128)(2,1)S(1)}, bf16[2,256,256]{2,1,0:T(8,128)(2,1)S(1)}, u32[]{:S(2)}, u32[]{:S(2)}) %collective-permute-start.40) | collective-permute-done | bytes 262176 | tf_op jit(solution)/shard_map/ppermute | solution.py:39
  173.3 0.8 add_convert_fusion
  (38 shorter events, 0.5 us)
Async XLA Ops:
  0.6 7.1 %copy-start = (bf16[2,256,256]{2,1,0:T(8,128)(2,1)S(1)}, bf16[2,256,256]{2,1,0:T(8,128)(2,1)}, u32[]{:S(2)}) copy-start(bf16[2,256,256]{2,1,0:T(8,128)(2,1)} %refs_12_.1) | copy-start | bytes 786436
  2.0 16.2 %collective-permute-start.1 = (bf16[256,512]{1,0:T(8,128)(2,1)S(1)}, bf16[256,512]{1,0:T(8,128)(2,1)S(1)}, u32[]{:S(2)}, u32[]{:S(2)}) collective-permute-start(bf16[256,512]{1,0:T(8,128)(2,1)S(1)} %get-tuple-element.52), channel_id=1, source_target_pairs={{0,4},{4,0},{8,12},{12,8},{1,5},{5,1},{9,13},{13,9},{2,6},{6,2},{1... | collective-permute-start | bytes 786440 | tf_op jit(solution)/shard_map/ppermute | solution.py:39
  5.1 27.0 %collective-permute-start.3 = (bf16[256,512]{1,0:T(8,128)(2,1)S(1)}, bf16[256,512]{1,0:T(8,128)(2,1)S(1)}, u32[]{:S(2)}, u32[]{:S(2)}) collective-permute-start(bf16[256,512]{1,0:T(8,128)(2,1)S(1)} %get-tuple-element.51), channel_id=1, source_target_pairs={{0,8},{4,12},{8,0},{12,4},{1,9},{5,13},{9,1},{13,5},{2,10},{6,14},... | collective-permute-start | bytes 786440 | tf_op jit(solution)/shard_map/ppermute | solution.py:39
  7.7 25.9 %collective-permute-start.5 = (bf16[256,512]{1,0:T(8,128)(2,1)S(1)}, bf16[256,512]{1,0:T(8,128)(2,1)S(1)}, u32[]{:S(2)}, u32[]{:S(2)}) collective-permute-start(bf16[256,512]{1,0:T(8,128)(2,1)S(1)} %get-tuple-element.50), channel_id=1, source_target_pairs={{0,12},{4,8},{8,4},{12,0},{1,13},{5,9},{9,5},{13,1},{2,14},{6,10},... | collective-permute-start | bytes 786440 | tf_op jit(solution)/shard_map/ppermute | solution.py:39
  7.7 34.3 %collective-permute-start.16 = (bf16[2,256,256]{2,1,0:T(8,128)(2,1)S(1)}, bf16[2,256,256]{2,1,0:T(8,128)(2,1)S(1)}, u32[]{:S(2)}, u32[]{:S(2)}) collective-permute-start(bf16[2,256,256]{2,1,0:T(8,128)(2,1)S(1)} %copy-done), channel_id=1, source_target_pairs={{0,8},{4,12},{8,0},{12,4},{1,9},{5,13},{9,1},{13,5},{2,10},{6,14},... | collective-permute-start | bytes 786440 | tf_op jit(solution)/shard_map/ppermute | solution.py:39
  9.6 32.4 %collective-permute-start.14 = (bf16[2,256,256]{2,1,0:T(8,128)(2,1)S(1)}, bf16[2,256,256]{2,1,0:T(8,128)(2,1)S(1)}, u32[]{:S(2)}, u32[]{:S(2)}) collective-permute-start(bf16[2,256,256]{2,1,0:T(8,128)(2,1)S(1)} %copy-done), channel_id=1, source_target_pairs={{0,4},{4,0},{8,12},{12,8},{1,5},{5,1},{9,13},{13,9},{2,6},{6,2},{1... | collective-permute-start | bytes 786440 | tf_op jit(solution)/shard_map/ppermute | solution.py:39
  18.2 26.3 %collective-permute-start = (bf16[256,512]{1,0:T(8,128)(2,1)S(1)}, bf16[256,512]{1,0:T(8,128)(2,1)S(1)}, u32[]{:S(2)}, u32[]{:S(2)}) collective-permute-start(bf16[256,512]{1,0:T(8,128)(2,1)S(1)} %get-tuple-element.53), channel_id=1, source_target_pairs={{0,16},{16,0},{1,17},{17,1},{2,18},{18,2},{3,19},{19,3},{4,20},{20... | collective-permute-start | bytes 786440 | tf_op jit(solution)/shard_map/ppermute | solution.py:34
  32.1 14.0 %collective-permute-start.13 = (bf16[2,256,256]{2,1,0:T(8,128)(2,1)S(1)}, bf16[2,256,256]{2,1,0:T(8,128)(2,1)S(1)}, u32[]{:S(2)}, u32[]{:S(2)}) collective-permute-start(bf16[2,256,256]{2,1,0:T(8,128)(2,1)S(1)} %copy-done), channel_id=1, source_target_pairs={{0,16},{16,0},{1,17},{17,1},{2,18},{18,2},{3,19},{19,3},{4,20},{20... | collective-permute-start | bytes 786440 | tf_op jit(solution)/shard_map/ppermute | solution.py:34
  33.6 14.4 %collective-permute-start.31 = (bf16[256,512]{1,0:T(8,128)(2,1)S(1)}, bf16[256,512]{1,0:T(8,128)(2,1)S(1)}, u32[]{:S(2)}, u32[]{:S(2)}) collective-permute-start(bf16[256,512]{1,0:T(8,128)(2,1)S(1)} %get-tuple-element.40), channel_id=1, source_target_pairs={{0,4},{4,0},{8,12},{12,8},{1,5},{5,1},{9,13},{13,9},{2,6},{6,2},{1... | collective-permute-start | bytes 786440 | tf_op jit(solution)/shard_map/ppermute | solution.py:39
  42.0 20.0 %collective-permute-start.32 = (bf16[256,512]{1,0:T(8,128)(2,1)S(1)}, bf16[256,512]{1,0:T(8,128)(2,1)S(1)}, u32[]{:S(2)}, u32[]{:S(2)}) collective-permute-start(bf16[256,512]{1,0:T(8,128)(2,1)S(1)} %get-tuple-element.41), channel_id=1, source_target_pairs={{0,8},{4,12},{8,0},{12,4},{1,9},{5,13},{9,1},{13,5},{2,10},{6,14},... | collective-permute-start | bytes 786440 | tf_op jit(solution)/shard_map/ppermute | solution.py:39
  42.0 21.5 %collective-permute-start.33 = (bf16[256,512]{1,0:T(8,128)(2,1)S(1)}, bf16[256,512]{1,0:T(8,128)(2,1)S(1)}, u32[]{:S(2)}, u32[]{:S(2)}) collective-permute-start(bf16[256,512]{1,0:T(8,128)(2,1)S(1)} %get-tuple-element.42), channel_id=1, source_target_pairs={{0,12},{4,8},{8,4},{12,0},{1,13},{5,9},{9,5},{13,1},{2,14},{6,10},... | collective-permute-start | bytes 786440 | tf_op jit(solution)/shard_map/ppermute | solution.py:39
  44.5 19.5 %collective-permute-start.21 = (bf16[256,512]{1,0:T(8,128)(2,1)S(1)}, bf16[256,512]{1,0:T(8,128)(2,1)S(1)}, u32[]{:S(2)}, u32[]{:S(2)}) collective-permute-start(bf16[256,512]{1,0:T(8,128)(2,1)S(1)} %collective-permute-done.1.refs_1_), channel_id=1, source_target_pairs={{0,2},{1,3},{2,0},{3,1},{4,6},{5,7},{6,4},{7,5},{8,10},{9,11},{10,... | collective-permute-start | bytes 786440 | tf_op jit(solution)/shard_map/ppermute | solution.py:52
  46.0 19.5 %collective-permute-start.22 = (bf16[256,512]{1,0:T(8,128)(2,1)S(1)}, bf16[256,512]{1,0:T(8,128)(2,1)S(1)}, u32[]{:S(2)}, u32[]{:S(2)}) collective-permute-start(bf16[256,512]{1,0:T(8,128)(2,1)S(1)} %collective-permute-done.3.refs_2_), channel_id=1, source_target_pairs={{0,2},{1,3},{2,0},{3,1},{4,6},{5,7},{6,4},{7,5},{8,10},{9,11},{10,... | collective-permute-start | bytes 786440 | tf_op jit(solution)/shard_map/ppermute | solution.py:52
  48.0 18.1 %collective-permute-start.4 = (bf16[256,512]{1,0:T(8,128)(2,1)S(1)}, bf16[256,512]{1,0:T(8,128)(2,1)S(1)}, u32[]{:S(2)}, u32[]{:S(2)}) collective-permute-start(bf16[256,512]{1,0:T(8,128)(2,1)S(1)} %collective-permute-done.3.refs_2_), channel_id=1, source_target_pairs={{0,16},{16,0},{1,17},{17,1},{2,18},{18,2},{3,19},{19,3},{4,20},{20... | collective-permute-start | bytes 786440 | tf_op jit(solution)/shard_map/ppermute | solution.py:34
  62.0 9.1 %collective-permute-start.6 = (bf16[256,512]{1,0:T(8,128)(2,1)S(1)}, bf16[256,512]{1,0:T(8,128)(2,1)S(1)}, u32[]{:S(2)}, u32[]{:S(2)}) collective-permute-start(bf16[256,512]{1,0:T(8,128)(2,1)S(1)} %collective-permute-done.5.refs_3_), channel_id=1, source_target_pairs={{0,16},{16,0},{1,17},{17,1},{2,18},{18,2},{3,19},{19,3},{4,20},{20... | collective-permute-start | bytes 786440 | tf_op jit(solution)/shard_map/ppermute | solution.py:34
  63.5 10.4 %collective-permute-start.2 = (bf16[256,512]{1,0:T(8,128)(2,1)S(1)}, bf16[256,512]{1,0:T(8,128)(2,1)S(1)}, u32[]{:S(2)}, u32[]{:S(2)}) collective-permute-start(bf16[256,512]{1,0:T(8,128)(2,1)S(1)} %collective-permute-done.1.refs_1_), channel_id=1, source_target_pairs={{0,16},{16,0},{1,17},{17,1},{2,18},{18,2},{3,19},{19,3},{4,20},{20... | collective-permute-start | bytes 786440 | tf_op jit(solution)/shard_map/ppermute | solution.py:34
  64.0 11.4 %collective-permute-start.23 = (bf16[256,512]{1,0:T(8,128)(2,1)S(1)}, bf16[256,512]{1,0:T(8,128)(2,1)S(1)}, u32[]{:S(2)}, u32[]{:S(2)}) collective-permute-start(bf16[256,512]{1,0:T(8,128)(2,1)S(1)} %collective-permute-done.5.refs_3_), channel_id=1, source_target_pairs={{0,2},{1,3},{2,0},{3,1},{4,6},{5,7},{6,4},{7,5},{8,10},{9,11},{10,... | collective-permute-start | bytes 786440 | tf_op jit(solution)/shard_map/ppermute | solution.py:52
  65.5 13.3 %collective-permute-start.8 = (bf16[256,512]{1,0:T(8,128)(2,1)S(1)}, bf16[256,512]{1,0:T(8,128)(2,1)S(1)}, u32[]{:S(2)}, u32[]{:S(2)}) collective-permute-start(bf16[256,512]{1,0:T(8,128)(2,1)S(1)} %collective-permute-done.refs_0_), channel_id=1, source_target_pairs={{0,2},{1,3},{2,0},{3,1},{4,6},{5,7},{6,4},{7,5},{8,10},{9,11},{10,... | collective-permute-start | bytes 786440 | tf_op jit(solution)/shard_map/ppermute | solution.py:52
  66.1 18.4 %collective-permute-start.10 = (bf16[256,512]{1,0:T(8,128)(2,1)S(1)}, bf16[256,512]{1,0:T(8,128)(2,1)S(1)}, u32[]{:S(2)}, u32[]{:S(2)}) collective-permute-start(bf16[256,512]{1,0:T(8,128)(2,1)S(1)} %collective-permute-done.4.refs_2_), channel_id=1, source_target_pairs={{0,2},{1,3},{2,0},{3,1},{4,6},{5,7},{6,4},{7,5},{8,10},{9,11},{10,... | collective-permute-start | bytes 786440 | tf_op jit(solution)/shard_map/ppermute | solution.py:52
  71.1 19.0 %collective-permute-start.11 = (bf16[256,512]{1,0:T(8,128)(2,1)S(1)}, bf16[256,512]{1,0:T(8,128)(2,1)S(1)}, u32[]{:S(2)}, u32[]{:S(2)}) collective-permute-start(bf16[256,512]{1,0:T(8,128)(2,1)S(1)} %collective-permute-done.6.refs_3_), channel_id=1, source_target_pairs={{0,2},{1,3},{2,0},{3,1},{4,6},{5,7},{6,4},{7,5},{8,10},{9,11},{10,... | collective-permute-start | bytes 786440 | tf_op jit(solution)/shard_map/ppermute | solution.py:52
  73.9 21.8 %collective-permute-start.9 = (bf16[256,512]{1,0:T(8,128)(2,1)S(1)}, bf16[256,512]{1,0:T(8,128)(2,1)S(1)}, u32[]{:S(2)}, u32[]{:S(2)}) collective-permute-start(bf16[256,512]{1,0:T(8,128)(2,1)S(1)} %collective-permute-done.2.refs_1_), channel_id=1, source_target_pairs={{0,2},{1,3},{2,0},{3,1},{4,6},{5,7},{6,4},{7,5},{8,10},{9,11},{10,... | collective-permute-start | bytes 786440 | tf_op jit(solution)/shard_map/ppermute | solution.py:52
  75.5 21.8 %collective-permute-start.18 = (bf16[2,256,256]{2,1,0:T(8,128)(2,1)S(1)}, bf16[2,256,256]{2,1,0:T(8,128)(2,1)S(1)}, u32[]{:S(2)}, u32[]{:S(2)}) collective-permute-start(bf16[2,256,256]{2,1,0:T(8,128)(2,1)S(1)} %collective-permute-done.16.refs_14_), channel_id=1, source_target_pairs={{0,4},{4,0},{8,12},{12,8},{1,5},{5,1},{9,13},{13,9},{2,6},{6,2},{1... | collective-permute-start | bytes 786440 | tf_op jit(solution)/shard_map/ppermute | solution.py:39
  78.8 18.5 %collective-permute-start.17 = (bf16[2,256,256]{2,1,0:T(8,128)(2,1)S(1)}, bf16[2,256,256]{2,1,0:T(8,128)(2,1)S(1)}, u32[]{:S(2)}, u32[]{:S(2)}) collective-permute-start(bf16[2,256,256]{2,1,0:T(8,128)(2,1)S(1)} %collective-permute-done.16.refs_14_), channel_id=1, source_target_pairs={{0,16},{16,0},{1,17},{17,1},{2,18},{18,2},{3,19},{19,3},{4,20},{20... | collective-permute-start | bytes 786440 | tf_op jit(solution)/shard_map/ppermute | solution.py:34
  84.5 16.2 %collective-permute-start.35 = (bf16[256,512]{1,0:T(8,128)(2,1)S(1)}, bf16[256,512]{1,0:T(8,128)(2,1)S(1)}, u32[]{:S(2)}, u32[]{:S(2)}) collective-permute-start(bf16[256,512]{1,0:T(8,128)(2,1)S(1)} %collective-permute-done.31.refs_1_), channel_id=1, source_target_pairs={{0,2},{1,3},{2,0},{3,1},{4,6},{5,7},{6,4},{7,5},{8,10},{9,11},{10,... | collective-permute-start | bytes 786440 | tf_op jit(solution)/shard_map/ppermute | solution.py:52
  90.1 26.1 %collective-permute-start.20 = (bf16[768,512]{1,0:T(8,128)(2,1)S(1)}, bf16[768,512]{1,0:T(8,128)(2,1)S(1)}, u32[]{:S(2)}, u32[]{:S(2)}) collective-permute-start(bf16[768,512]{1,0:T(8,128)(2,1)S(1)} %pad_maximum_fusion.2), channel_id=1, source_target_pairs={{0,1},{1,0},{2,3},{3,2},{4,5},{5,4},{6,7},{7,6},{8,9},{9,8},{10,11... | collective-permute-start | bytes 2359304 | tf_op jit(solution)/shard_map/ppermute | solution.py:52
  95.7 7.8 %collective-permute-start.36 = (bf16[256,512]{1,0:T(8,128)(2,1)S(1)}, bf16[256,512]{1,0:T(8,128)(2,1)S(1)}, u32[]{:S(2)}, u32[]{:S(2)}) collective-permute-start(bf16[256,512]{1,0:T(8,128)(2,1)S(1)} %collective-permute-done.32.refs_2_), channel_id=1, source_target_pairs={{0,2},{1,3},{2,0},{3,1},{4,6},{5,7},{6,4},{7,5},{8,10},{9,11},{10,... | collective-permute-start | bytes 786440 | tf_op jit(solution)/shard_map/ppermute | solution.py:52
  97.3 19.5 %collective-permute-start.24 = (bf16[768,512]{1,0:T(8,128)(2,1)S(1)}, bf16[768,512]{1,0:T(8,128)(2,1)S(1)}, u32[]{:S(2)}, u32[]{:S(2)}) collective-permute-start(bf16[768,512]{1,0:T(8,128)(2,1)S(1)} %pad_maximum_fusion.3), channel_id=1, source_target_pairs={{0,1},{1,0},{2,3},{3,2},{4,5},{5,4},{6,7},{7,6},{8,9},{9,8},{10,11... | collective-permute-start | bytes 2359304 | tf_op jit(solution)/shard_map/ppermute | solution.py:52
  97.4 27.6 %collective-permute-start.7 = (bf16[1024,512]{1,0:T(8,128)(2,1)S(1)}, bf16[1024,512]{1,0:T(8,128)(2,1)S(1)}, u32[]{:S(2)}, u32[]{:S(2)}) collective-permute-start(bf16[1024,512]{1,0:T(8,128)(2,1)S(1)} %pad_maximum_fusion), channel_id=1, source_target_pairs={{0,1},{1,0},{2,3},{3,2},{4,5},{5,4},{6,7},{7,6},{8,9},{9,8},{10,11... | collective-permute-start | bytes 3145736 | tf_op jit(solution)/shard_map/ppermute | solution.py:52
  100.7 24.4 %collective-permute-start.12 = (bf16[1024,512]{1,0:T(8,128)(2,1)S(1)}, bf16[1024,512]{1,0:T(8,128)(2,1)S(1)}, u32[]{:S(2)}, u32[]{:S(2)}) collective-permute-start(bf16[1024,512]{1,0:T(8,128)(2,1)S(1)} %pad_maximum_fusion.1), channel_id=1, source_target_pairs={{0,1},{1,0},{2,3},{3,2},{4,5},{5,4},{6,7},{7,6},{8,9},{9,8},{10,11... | collective-permute-start | bytes 3145736 | tf_op jit(solution)/shard_map/ppermute | solution.py:52
  103.5 6.4 %collective-permute-start.37 = (bf16[256,512]{1,0:T(8,128)(2,1)S(1)}, bf16[256,512]{1,0:T(8,128)(2,1)S(1)}, u32[]{:S(2)}, u32[]{:S(2)}) collective-permute-start(bf16[256,512]{1,0:T(8,128)(2,1)S(1)} %collective-permute-done.33.refs_3_), channel_id=1, source_target_pairs={{0,2},{1,3},{2,0},{3,1},{4,6},{5,7},{6,4},{7,5},{8,10},{9,11},{10,... | collective-permute-start | bytes 786440 | tf_op jit(solution)/shard_map/ppermute | solution.py:52
  109.8 6.4 %collective-permute-start.15 = (bf16[2,256,256]{2,1,0:T(8,128)(2,1)S(1)}, bf16[2,256,256]{2,1,0:T(8,128)(2,1)S(1)}, u32[]{:S(2)}, u32[]{:S(2)}) collective-permute-start(bf16[2,256,256]{2,1,0:T(8,128)(2,1)S(1)} %collective-permute-done.14.refs_13_), channel_id=1, source_target_pairs={{0,16},{16,0},{1,17},{17,1},{2,18},{18,2},{3,19},{19,3},{4,20},{20... | collective-permute-start | bytes 786440 | tf_op jit(solution)/shard_map/ppermute | solution.py:34
  116.2 27.9 %collective-permute-start.34 = (bf16[768,512]{1,0:T(8,128)(2,1)S(1)}, bf16[768,512]{1,0:T(8,128)(2,1)S(1)}, u32[]{:S(2)}, u32[]{:S(2)}) collective-permute-start(bf16[768,512]{1,0:T(8,128)(2,1)S(1)} %pad_maximum_fusion.4), channel_id=1, source_target_pairs={{0,1},{1,0},{2,3},{3,2},{4,5},{5,4},{6,7},{7,6},{8,9},{9,8},{10,11... | collective-permute-start | bytes 2359304 | tf_op jit(solution)/shard_map/ppermute | solution.py:52
  116.2 27.9 %collective-permute-start.38 = (bf16[768,512]{1,0:T(8,128)(2,1)S(1)}, bf16[768,512]{1,0:T(8,128)(2,1)S(1)}, u32[]{:S(2)}, u32[]{:S(2)}) collective-permute-start(bf16[768,512]{1,0:T(8,128)(2,1)S(1)} %pad_maximum_fusion.5), channel_id=1, source_target_pairs={{0,1},{1,0},{2,3},{3,2},{4,5},{5,4},{6,7},{7,6},{8,9},{9,8},{10,11... | collective-permute-start | bytes 2359304 | tf_op jit(solution)/shard_map/ppermute | solution.py:52
  116.7 8.3 %collective-permute-start.19 = (bf16[2,256,256]{2,1,0:T(8,128)(2,1)S(1)}, bf16[2,256,256]{2,1,0:T(8,128)(2,1)S(1)}, u32[]{:S(2)}, u32[]{:S(2)}) collective-permute-start(bf16[2,256,256]{2,1,0:T(8,128)(2,1)S(1)} %collective-permute-done.18.refs_15_), channel_id=1, source_target_pairs={{0,16},{16,0},{1,17},{17,1},{2,18},{18,2},{3,19},{19,3},{4,20},{20... | collective-permute-start | bytes 786440 | tf_op jit(solution)/shard_map/ppermute | solution.py:34
  128.2 10.3 %collective-permute-start.25 = (f32[8,128]{1,0:T(8,128)S(1)}, f32[8,128]{1,0:T(8,128)S(1)}, u32[]{:S(2)}, u32[]{:S(2)}) collective-permute-start(f32[8,128]{1,0:T(8,128)S(1)} %get-tuple-element.31), channel_id=1, source_target_pairs={{0,4},{4,8},{8,12},{12,0},{1,5},{5,9},{9,13},{13,1},{2,6},{6,10},{... | collective-permute-start | bytes 12296 | tf_op jit(solution)/shard_map/ppermute | solution.py:34
  134.2 4.5 %collective-permute-start.26 = (f32[8,128]{1,0:T(8,128)S(1)}, f32[8,128]{1,0:T(8,128)S(1)}, u32[]{:S(2)}, u32[]{:S(2)}) collective-permute-start(f32[8,128]{1,0:T(8,128)S(1)} %get-tuple-element.31), channel_id=1, source_target_pairs={{0,8},{4,12},{8,0},{12,4},{1,9},{5,13},{9,1},{13,5},{2,10},{6,14},... | collective-permute-start | bytes 12296 | tf_op jit(solution)/shard_map/ppermute | solution.py:34
  135.6 4.2 %collective-permute-start.27 = (f32[8,128]{1,0:T(8,128)S(1)}, f32[8,128]{1,0:T(8,128)S(1)}, u32[]{:S(2)}, u32[]{:S(2)}) collective-permute-start(f32[8,128]{1,0:T(8,128)S(1)} %get-tuple-element.31), channel_id=1, source_target_pairs={{0,12},{4,0},{8,4},{12,8},{1,13},{5,1},{9,5},{13,9},{2,14},{6,2},{... | collective-permute-start | bytes 12296 | tf_op jit(solution)/shard_map/ppermute | solution.py:34
  139.8 3.0 %collective-permute-start.28 = (f32[8,128]{1,0:T(8,128)S(1)}, f32[8,128]{1,0:T(8,128)S(1)}, u32[]{:S(2)}, u32[]{:S(2)}) collective-permute-start(f32[8,128]{1,0:T(8,128)S(1)} %add_add_fusion.1), channel_id=1, source_target_pairs={{0,1},{1,2},{2,3},{3,0},{4,5},{5,6},{6,7},{7,4},{8,9},{9,10},{10,1... | collective-permute-start | bytes 12296 | tf_op jit(solution)/shard_map/ppermute | solution.py:34
  139.8 3.6 %collective-permute-start.29 = (f32[8,128]{1,0:T(8,128)S(1)}, f32[8,128]{1,0:T(8,128)S(1)}, u32[]{:S(2)}, u32[]{:S(2)}) collective-permute-start(f32[8,128]{1,0:T(8,128)S(1)} %add_add_fusion.1), channel_id=1, source_target_pairs={{0,2},{1,3},{2,0},{3,1},{4,6},{5,7},{6,4},{7,5},{8,10},{9,11},{10,... | collective-permute-start | bytes 12296 | tf_op jit(solution)/shard_map/ppermute | solution.py:34
  141.3 2.8 %collective-permute-start.30 = (f32[8,128]{1,0:T(8,128)S(1)}, f32[8,128]{1,0:T(8,128)S(1)}, u32[]{:S(2)}, u32[]{:S(2)}) collective-permute-start(f32[8,128]{1,0:T(8,128)S(1)} %add_add_fusion.1), channel_id=1, source_target_pairs={{0,3},{1,0},{2,1},{3,2},{4,7},{5,4},{6,5},{7,6},{8,11},{9,8},{10,9... | collective-permute-start | bytes 12296 | tf_op jit(solution)/shard_map/ppermute | solution.py:34
  150.2 14.2 %collective-permute-start.39 = (bf16[2,256,256]{2,1,0:T(8,128)(2,1)S(1)}, bf16[2,256,256]{2,1,0:T(8,128)(2,1)S(1)}, u32[]{:S(2)}, u32[]{:S(2)}) collective-permute-start(bf16[2,256,256]{2,1,0:T(8,128)(2,1)S(1)} %get-tuple-element.47), channel_id=1, source_target_pairs={{0,4},{4,0},{8,12},{12,8},{1,5},{5,1},{9,13},{13,9},{2,6},{6,2},{1... | collective-permute-start | bytes 786440 | tf_op jit(solution)/shard_map/ppermute | solution.py:39
  151.1 22.2 %collective-permute-start.40 = (bf16[2,256,256]{2,1,0:T(8,128)(2,1)S(1)}, bf16[2,256,256]{2,1,0:T(8,128)(2,1)S(1)}, u32[]{:S(2)}, u32[]{:S(2)}) collective-permute-start(bf16[2,256,256]{2,1,0:T(8,128)(2,1)S(1)} %get-tuple-element.48), channel_id=1, source_target_pairs={{0,8},{4,12},{8,0},{12,4},{1,9},{5,13},{9,1},{13,5},{2,10},{6,14},... | collective-permute-start | bytes 786440 | tf_op jit(solution)/shard_map/ppermute | solution.py:39
  154.9 18.4 %collective-permute-start.41 = (bf16[2,256,256]{2,1,0:T(8,128)(2,1)S(1)}, bf16[2,256,256]{2,1,0:T(8,128)(2,1)S(1)}, u32[]{:S(2)}, u32[]{:S(2)}) collective-permute-start(bf16[2,256,256]{2,1,0:T(8,128)(2,1)S(1)} %get-tuple-element.49), channel_id=1, source_target_pairs={{0,12},{4,8},{8,4},{12,0},{1,13},{5,9},{9,5},{13,1},{2,14},{6,10},... | collective-permute-start | bytes 786440 | tf_op jit(solution)/shard_map/ppermute | solution.py:39

commit v2 on v1

--- a/solution.py
+++ b/solution.py
@@ -107,10 +107,19 @@
     return (new_master, new_first, new_second)
 
 
-def project_kernel(sizes, rows, n_f, count, at_ref, squares_ref, grad_ref, master_ref, m_ref, v_ref, *refs):
-    tokens, refs = split(refs, sizes)
-    outs, weight = refs[:n_f], refs[n_f]
-    chunk, shard = tokens[0][0].shape[1], weight.shape[1]
+def project_rows(at, tokens, weight, s):
+    chunk = tokens[0].shape[1]
+    acc = None
+    for r, block in enumerate(tokens):
+        part = pl.ds(pl.multiple_of((at ^ r) * chunk, chunk), chunk)
+        term = jnp.dot(block, weight[s, part, :], preferred_element_type=jnp.float32)
+        acc = term if acc is None else acc + term
+    return acc
+
+
+def project_kernel(n_t, count, at_ref, squares_ref, grad_ref, master_ref, m_ref, v_ref, *refs):
+    tokens, (weight, out) = refs[:n_t], refs[n_t:]
+    shard = weight.shape[1]
     block = min(shard, 128)
     scale = clip_scale(squares_ref[...], count)
     for s in range(2):
@@ -123,13 +132,15 @@
             return carry
 
         lax.fori_loop(0, shard // block, update_block, 0)
-        blocks = [row_blocks(group, rows) for group in tokens]
-        for k in range(n_f):
-            acc = jnp.zeros(outs[0].shape[1:], jnp.float32)
-            for r, group in enumerate(blocks):
-                at = pl.multiple_of((at_ref[0] ^ r) * chunk, chunk)
-                acc += jnp.dot(group[k], weight[s, pl.ds(at, chunk), :], preferred_element_type=jnp.float32)
-            outs[k][s] = acc.astype(outs[k].dtype)
+        out[s] = project_rows(at_ref[0], [ref[...] for ref in tokens], weight, s).astype(out.dtype)
+
+
+def finish_kernel(sizes, rows, at_ref, weight, *refs):
+    tokens, outs = split(refs, sizes)
+    blocks = [row_blocks(group, rows) for group in tokens]
+    for s in range(2):
+        for k, out in enumerate(outs):
+            out[s] = project_rows(at_ref[0], [group[k] for group in blocks], weight, s).astype(out.dtype)
 
 
 def stage_kernel(plan, at_ref, *refs):
@@ -219,7 +230,10 @@
         bit = k & -k
         cots.append(trade(cots[k ^ bit], "fsdp", bit))
     other_cots = [shift(c, "dp", 1) for c in cots]
-    next_rest = spread(fetch(next_others), "tensor")
+    next_others = fetch(next_others)
+    lead = n_f // 2
+    next_lead = spread([next_others.pop(lead - 1)], "tensor")
+    next_rest = spread(next_others, "tensor")
 
     def flat(groups):
         return [near(piece) for group in groups for piece in group], [len(group) for group in groups]
@@ -241,22 +255,29 @@
         compiler_params=PARAMS,
     )(at, *tokens_in, *map(near, other_cots), grad)
 
-    for axis, n in (("fsdp", n_f), ("tensor", n_t)):
+    for axis, n in (("tensor", n_t), ("fsdp", n_f)):
         squares = functools.reduce(jnp.add, [shift(squares, axis, k) for k in range(1, n)], squares)
 
-    out = (2, rows, kv)
-    tokens_in, sizes = flat([[a] + b for a, b in zip(next_first, next_rest, strict=True)])
-    partial = pl.pallas_call(
-        functools.partial(project_kernel, sizes, rows, n_f, count),
-        out_shape=(jax.ShapeDtypeStruct(out, jnp.float32),)
-        + (jax.ShapeDtypeStruct(out, jnp.bfloat16),) * (n_f - 1),
-        in_specs=[SMEM] + [VMEM] * (5 + len(tokens_in)),
-        out_specs=(VMEM,) * n_f,
-        scratch_shapes=[pltpu.VMEM((2, shard, kv), jnp.bfloat16)],
+    out = jax.ShapeDtypeStruct((2, rows, kv), jnp.bfloat16)
+    tokens_in, _ = flat(next_lead)
+    weight, lead_partial = pl.pallas_call(
+        functools.partial(project_kernel, n_t, count),
+        out_shape=(pltpu.VMEM(shard_shape, jnp.bfloat16), out),
+        in_specs=[SMEM] + [VMEM] * (5 + n_t),
+        out_specs=(VMEM, VMEM),
         compiler_params=PARAMS,
     )(at, squares, grad, *state, *tokens_in)
-    got = [trade(partial[k], "fsdp", k) for k in range(1, n_f)]
-    projected = functools.reduce(jnp.add, [g.astype(jnp.float32) for g in got], partial[0])
+    tokens_in, sizes = flat([[a] + b for a, b in zip(next_first, next_rest, strict=True)])
+    own, *partial = pl.pallas_call(
+        functools.partial(finish_kernel, sizes, rows),
+        out_shape=(jax.ShapeDtypeStruct(out.shape, jnp.float32),) + (out,) * (n_f - 2),
+        in_specs=[SMEM] + [VMEM] * (1 + len(tokens_in)),
+        out_specs=(VMEM,) * (n_f - 1),
+        compiler_params=PARAMS,
+    )(at, weight, *tokens_in)
+    partial.insert(lead - 1, lead_partial)
+    got = [trade(x, "fsdp", k) for k, x in enumerate(partial, 1)]
+    projected = functools.reduce(jnp.add, [g.astype(jnp.float32) for g in got], own)
     copies = 3 * 2 * (shard // min(shard, 512))
     new_master, new_first, new_second = pl.pallas_call(
         functools.partial(update_kernel, count),

time: 177 us -> 170 us (0.960); the launches traced: 174 us -> 170 us
  starting transfers between devices: 62.9 us -> 46.7 us
  waiting for transfers between devices: 84.5 us -> 95.4 us
    ppermute x14, waiting for transfers between devices: 16 us -> 27.1 us  [shift(): return lax.ppermute(x, axis, [(i, (i + k) % n) for i in range(n)])]
    ppermute x14, starting transfers between devices: 24.4 us -> 13.4 us  [shift(): return lax.ppermute(x, axis, [(i, (i + k) % n) for i in range(n)])]
    ppermute x12, starting transfers between devices: 24.3 us -> 17.7 us  [trade(): return lax.ppermute(x, axis, [(i, i ^ k) for i in range(n)])]
    ppermute x16 -> x18, starting transfers between devices: 14.1 us -> 15.6 us  [spread(): moved.append(lax.ppermute(piece, axis, [(j, j ^ stride) for j in range(n)]))]
    pallas_call x1 -> x2, Pallas kernels: 6.05 us -> 7.2 us  [the longest x1 4.86 us: per_device(): pl.pallas_call(functools.partial(project_kernel, n_t, count), out_shape=(...]
    ppermute x16 -> x18, waiting for transfers between devices: 25.3 us -> 24.9 us  [spread(): moved.append(lax.ppermute(piece, axis, [(j, j ^ stride) for j in range(n)]))]
  transfers between devices with their start and end apart: 42 -> 44, of which waited for: 22 -> 23; matrix products, arithmetic and copies ran while one was open for 0% -> 0% of each run, Pallas kernels for 10% -> 13%
where the time goes in v2:
time: 170 us
  waiting for transfers between devices  95.4 us (56%)
  starting transfers between devices  46.7 us (27%)
  Pallas kernels  24.6 us (14%)
    ppermute x12, waiting for transfers between devices, trade(): return lax.ppermute(x, axis, [(i, i ^ k) for i in range(n)])  43.3 us
    ppermute x14, waiting for transfers between devices, shift(): return lax.ppermute(x, axis, [(i, (i + k) % n) for i in range(n)])  27.1 us
    ppermute x18, waiting for transfers between devices, spread(): moved.append(lax.ppermute(piece, axis, [(j, j ^ stride) for j in range(n)]))  24.9 us
    ppermute x12, starting transfers between devices, trade(): return lax.ppermute(x, axis, [(i, i ^ k) for i in range(n)])  17.7 us
    ppermute x18, starting transfers between devices, spread(): moved.append(lax.ppermute(piece, axis, [(j, j ^ stride) for j in range(n)]))  15.6 us
    ppermute x14, starting transfers between devices, shift(): return lax.ppermute(x, axis, [(i, (i + k) % n) for i in range(n)])  13.4 us
    pallas_call x1, Pallas kernels, per_device(): pl.pallas_call(functools.partial(stage_kernel, Plan(5, n_t, tuple(outs)))...  6.03 us
    pallas_call x1, Pallas kernels, per_device(): pl.pallas_call(functools.partial(update_kernel, count), out_shape=(jax.Sh...  5.22 us
  transfers between devices with their start and end apart: 44, of which 23 were waited for; matrix products, arithmetic and copies ran while one was open for 0% of the time, Pallas kernels for 13%

profile of v2, /device:TPU:0, one launch (start us, length us, event | category | flops | bytes accessed | tf_op | source)
XLA Modules:
  0.0 170.1 jit_solution(59542841818362472)
XLA Ops:
  0.7 1.3 constant_dynamic-slice_fusion
  2.0 3.1 %collective-permute-start.1 = (bf16[256,512]{1,0:T(8,128)(2,1)S(1)}, bf16[256,512]{1,0:T(8,128)(2,1)S(1)}, u32[]{:S(2)}, u32[]{:S(2)}) collective-permute-start(bf16[256,512]{1,0:T(8,128)(2,1)S(1)} %get-tuple-element.54), channel_id=1, source_target_pairs={{0,4},{4,0},{8,12},{12,8},{1,5},{5,1},{9,13},{13,9},{2,6},{6,2},{1... | collective-permute-start | bytes 786440 | tf_op jit(solution)/shard_map/ppermute | solution.py:39
  5.1 2.6 %collective-permute-start.3 = (bf16[256,512]{1,0:T(8,128)(2,1)S(1)}, bf16[256,512]{1,0:T(8,128)(2,1)S(1)}, u32[]{:S(2)}, u32[]{:S(2)}) collective-permute-start(bf16[256,512]{1,0:T(8,128)(2,1)S(1)} %get-tuple-element.53), channel_id=1, source_target_pairs={{0,8},{4,12},{8,0},{12,4},{1,9},{5,13},{9,1},{13,5},{2,10},{6,14},... | collective-permute-start | bytes 786440 | tf_op jit(solution)/shard_map/ppermute | solution.py:39
  7.7 1.9 %collective-permute-start.16 = (bf16[2,256,256]{2,1,0:T(8,128)(2,1)S(1)}, bf16[2,256,256]{2,1,0:T(8,128)(2,1)S(1)}, u32[]{:S(2)}, u32[]{:S(2)}) collective-permute-start(bf16[2,256,256]{2,1,0:T(8,128)(2,1)S(1)} %copy-done), channel_id=1, source_target_pairs={{0,8},{4,12},{8,0},{12,4},{1,9},{5,13},{9,1},{13,5},{2,10},{6,14},... | collective-permute-start | bytes 786440 | tf_op jit(solution)/shard_map/ppermute | solution.py:39
  9.6 2.5 %collective-permute-start.14 = (bf16[2,256,256]{2,1,0:T(8,128)(2,1)S(1)}, bf16[2,256,256]{2,1,0:T(8,128)(2,1)S(1)}, u32[]{:S(2)}, u32[]{:S(2)}) collective-permute-start(bf16[2,256,256]{2,1,0:T(8,128)(2,1)S(1)} %copy-done), channel_id=1, source_target_pairs={{0,4},{4,0},{8,12},{12,8},{1,5},{5,1},{9,13},{13,9},{2,6},{6,2},{1... | collective-permute-start | bytes 786440 | tf_op jit(solution)/shard_map/ppermute | solution.py:39
  12.1 5.1 %collective-permute-done.1.refs_1_ = bf16[256,512]{1,0:T(8,128)(2,1)S(1)} collective-permute-done((bf16[256,512]{1,0:T(8,128)(2,1)S(1)}, bf16[256,512]{1,0:T(8,128)(2,1)S(1)}, u32[]{:S(2)}, u32[]{:S(2)}) %collective-permute-start.1) | collective-permute-done | bytes 262176 | tf_op jit(solution)/shard_map/ppermute | solution.py:39
  17.1 2.0 %collective-permute-start = (bf16[256,512]{1,0:T(8,128)(2,1)S(1)}, bf16[256,512]{1,0:T(8,128)(2,1)S(1)}, u32[]{:S(2)}, u32[]{:S(2)}) collective-permute-start(bf16[256,512]{1,0:T(8,128)(2,1)S(1)} %get-tuple-element.55), channel_id=1, source_target_pairs={{0,16},{16,0},{1,17},{17,1},{2,18},{18,2},{3,19},{19,3},{4,20},{20... | collective-permute-start | bytes 786440 | tf_op jit(solution)/shard_map/ppermute | solution.py:34
  19.2 12.9 %collective-permute-done.3.refs_2_ = bf16[256,512]{1,0:T(8,128)(2,1)S(1)} collective-permute-done((bf16[256,512]{1,0:T(8,128)(2,1)S(1)}, bf16[256,512]{1,0:T(8,128)(2,1)S(1)}, u32[]{:S(2)}, u32[]{:S(2)}) %collective-permute-start.3) | collective-permute-done | bytes 262176 | tf_op jit(solution)/shard_map/ppermute | solution.py:39
  32.1 1.5 collective-permute-start.13
  33.6 6.0 %shard_map.93 = (f32[2,2048,256]{2,1,0:T(8,128)S(1)}, f32[2,2048,256]{2,1,0:T(8,128)S(1)}, f32[2,2048,256]{2,1,0:T(8,128)S(1)}, bf16[256,512]{1,0:T(8,128)(2,1)S...) custom-call(s32[2]{0:T(128)S(1)} %pad_add_fusion.at_ref, ...), custom_call_target="tpu_custom_call" | custom-call | tf_op jit(solution)/shard_map/pallas_call | solution.py:210
  39.7 9.2 %collective-permute-done.16.refs_14_ = bf16[2,256,256]{2,1,0:T(8,128)(2,1)S(1)} collective-permute-done((bf16[2,256,256]{2,1,0:T(8,128)(2,1)S(1)}, bf16[2,256,256]{2,1,0:T(8,128)(2,1)S(1)}, u32[]{:S(2)}, u32[]{:S(2)}) %collective-permute-start.16) | collective-permute-done | bytes 262176 | tf_op jit(solution)/shard_map/ppermute | solution.py:39
  48.9 1.5 collective-permute-start.4
  50.4 0.5 collective-permute-start.6
  51.0 1.5 collective-permute-start.2
  52.5 0.8 collective-permute-done.31.refs_0_
  53.3 1.5 collective-permute-start.8
  54.8 3.3 %collective-permute-done.4.refs_2_ = bf16[256,512]{1,0:T(8,128)(2,1)S(1)} collective-permute-done((bf16[256,512]{1,0:T(8,128)(2,1)S(1)}, bf16[256,512]{1,0:T(8,128)(2,1)S(1)}, u32[]{:S(2)}, u32[]{:S(2)}) %collective-permute-start.4) | collective-permute-done | bytes 262176 | tf_op jit(solution)/shard_map/ppermute | solution.py:34
  58.1 1.5 collective-permute-start.10
  59.6 3.1 %collective-permute-done.6.refs_3_ = bf16[256,512]{1,0:T(8,128)(2,1)S(1)} collective-permute-done((bf16[256,512]{1,0:T(8,128)(2,1)S(1)}, bf16[256,512]{1,0:T(8,128)(2,1)S(1)}, u32[]{:S(2)}, u32[]{:S(2)}) %collective-permute-start.6) | collective-permute-done | bytes 262176 | tf_op jit(solution)/shard_map/ppermute | solution.py:34
  62.7 1.5 collective-permute-start.11
  64.2 1.3 collective-permute-done.2.refs_1_
  65.5 1.5 collective-permute-start.9
  67.0 2.7 %collective-permute-start.36 = (bf16[256,512]{1,0:T(8,128)(2,1)S(1)}, bf16[256,512]{1,0:T(8,128)(2,1)S(1)}, u32[]{:S(2)}, u32[]{:S(2)}) collective-permute-start(bf16[256,512]{1,0:T(8,128)(2,1)S(1)} %get-tuple-element.44), channel_id=1, source_target_pairs={{0,12},{4,8},{8,4},{12,0},{1,13},{5,9},{9,5},{13,1},{2,14},{6,10},... | collective-permute-start | bytes 786440 | tf_op jit(solution)/shard_map/ppermute | solution.py:39
  69.7 0.5 collective-permute-start.21
  70.3 1.5 collective-permute-start.22
  71.7 1.9 %collective-permute-done.11.refs_8_ = bf16[256,512]{1,0:T(8,128)(2,1)S(1)} collective-permute-done((bf16[256,512]{1,0:T(8,128)(2,1)S(1)}, bf16[256,512]{1,0:T(8,128)(2,1)S(1)}, u32[]{:S(2)}, u32[]{:S(2)}) %collective-permute-start.11) | collective-permute-done | bytes 262176 | tf_op jit(solution)/shard_map/ppermute | solution.py:52
  73.7 1.5 collective-permute-start.23
  75.2 4.1 %collective-permute-done.9.refs_6_ = bf16[256,512]{1,0:T(8,128)(2,1)S(1)} collective-permute-done((bf16[256,512]{1,0:T(8,128)(2,1)S(1)}, bf16[256,512]{1,0:T(8,128)(2,1)S(1)}, u32[]{:S(2)}, u32[]{:S(2)}) %collective-permute-start.9) | collective-permute-done | bytes 262176 | tf_op jit(solution)/shard_map/ppermute | solution.py:52
  79.3 1.2 collective-permute-start.18
  80.7 0.6 collective-permute-start.17
  81.3 3.6 %collective-permute-done.21.refs_7_ = bf16[256,512]{1,0:T(8,128)(2,1)S(1)} collective-permute-done((bf16[256,512]{1,0:T(8,128)(2,1)S(1)}, bf16[256,512]{1,0:T(8,128)(2,1)S(1)}, u32[]{:S(2)}, u32[]{:S(2)}) %collective-permute-start.21) | collective-permute-done | bytes 262176 | tf_op jit(solution)/shard_map/ppermute | solution.py:52
  84.9 1.5 collective-permute-start.15
  86.4 4.1 %collective-permute-done.22.refs_8_ = bf16[256,512]{1,0:T(8,128)(2,1)S(1)} collective-permute-done((bf16[256,512]{1,0:T(8,128)(2,1)S(1)}, bf16[256,512]{1,0:T(8,128)(2,1)S(1)}, u32[]{:S(2)}, u32[]{:S(2)}) %collective-permute-start.22) | collective-permute-done | bytes 262176 | tf_op jit(solution)/shard_map/ppermute | solution.py:52
  90.5 1.5 collective-permute-start.38
  92.0 4.1 %collective-permute-done.23.refs_9_ = bf16[256,512]{1,0:T(8,128)(2,1)S(1)} collective-permute-done((bf16[256,512]{1,0:T(8,128)(2,1)S(1)}, bf16[256,512]{1,0:T(8,128)(2,1)S(1)}, u32[]{:S(2)}, u32[]{:S(2)}) %collective-permute-start.23) | collective-permute-done | bytes 262176 | tf_op jit(solution)/shard_map/ppermute | solution.py:52
  96.2 0.5 collective-permute-start.12
  96.9 0.5 collective-permute-start.24
  97.4 2.1 %collective-permute-done.38.refs_6_ = bf16[256,512]{1,0:T(8,128)(2,1)S(1)} collective-permute-done((bf16[256,512]{1,0:T(8,128)(2,1)S(1)}, bf16[256,512]{1,0:T(8,128)(2,1)S(1)}, u32[]{:S(2)}, u32[]{:S(2)}) %collective-permute-start.38) | collective-permute-done | bytes 262176 | tf_op jit(solution)/shard_map/ppermute | solution.py:52
  99.4 1.5 collective-permute-start.39
  100.9 4.9 %collective-permute-done.39.refs_7_ = bf16[256,512]{1,0:T(8,128)(2,1)S(1)} collective-permute-done((bf16[256,512]{1,0:T(8,128)(2,1)S(1)}, bf16[256,512]{1,0:T(8,128)(2,1)S(1)}, u32[]{:S(2)}, u32[]{:S(2)}) %collective-permute-start.39) | collective-permute-done | bytes 262176 | tf_op jit(solution)/shard_map/ppermute | solution.py:52
  105.8 1.5 collective-permute-start.19
  107.3 4.9 %collective-permute-done.19.refs_13_ = bf16[2,256,256]{2,1,0:T(8,128)(2,1)S(1)} collective-permute-done((bf16[2,256,256]{2,1,0:T(8,128)(2,1)S(1)}, bf16[2,256,256]{2,1,0:T(8,128)(2,1)S(1)}, u32[]{:S(2)}, u32[]{:S(2)}) %collective-permute-start.19) | collective-permute-done | bytes 262176 | tf_op jit(solution)/shard_map/ppermute | solution.py:34
  112.2 1.5 collective-permute-start.33
  113.9 0.5 collective-permute-start.40
  114.4 2.9 %shard_map.94.refs_14_ = f32[2,2048,256]{2,1,0:T(8,128)S(1)} custom-call(s32[2]{0:T(128)S(1)} %pad_add_fusion.at_ref, bf16[256,512]{1,0:T(8,128)(2,1)S(1)} %get-tuple-element.28.refs_0_, bf16[256,512]{1,0:T(8,128)(2,1)S(1)} %collective-permute-done.1.refs_1_, bf16[256,512]{1,0:T(8,128)(2,1)S(1)} %collective-permute-done.3.refs_2_, ...), custom_call_target="tpu_custom_call" | custom-call | tf_op jit(solution)/shard_map/pallas_call | solution.py:242
  117.3 3.2 %shard_map.95 = (f32[2,2048,256]{2,1,0:T(8,128)S(1)}, f32[8,128]{1,0:T(8,128)S(1)}) custom-call(s32[2]{0:T(128)S(1)} %pad_add_fusion.at_ref, bf16[256,512]{1,0:T(8,128)(2,1)S(1)} %collective-permute-done.refs_0_, bf16[256,512]{1,0:T(8,128)(2,1)S(1)} %collective-permute-done.2.refs_1_, bf16[256,512]{1,0:T(8,128)(2,1)S(1)} %collective-permute-done.4.refs_2_, ...), custom_call_target="tpu_custom_call" | custom-call | tf_op jit(solution)/shard_map/pallas_call | solution.py:250
  120.5 0.1 collective-permute-start.25
  120.7 0.5 collective-permute-start.26
  121.2 1.4 collective-permute-start.27
  122.6 1.0 collective-permute-done.25
  123.6 0.7 collective-permute-done.26
  124.3 5.4 %collective-permute-done.28 = f32[8,128]{1,0:T(8,128)S(1)} collective-permute-done((f32[8,128]{1,0:T(8,128)S(1)}, f32[8,128]{1,0:T(8,128)S(1)}, u32[]{:S(2)}, u32[]{:S(2)}) %collective-permute-start.28) | collective-permute-done | bytes 4128 | tf_op jit(solution)/shard_map/ppermute | solution.py:34
  129.7 4.5 %collective-permute-done.29 = f32[8,128]{1,0:T(8,128)S(1)} collective-permute-done((f32[8,128]{1,0:T(8,128)S(1)}, f32[8,128]{1,0:T(8,128)S(1)}, u32[]{:S(2)}, u32[]{:S(2)}) %collective-permute-start.29) | collective-permute-done | bytes 4128 | tf_op jit(solution)/shard_map/ppermute | solution.py:34
  134.2 0.7 collective-permute-start.30
  134.9 2.9 %collective-permute-done.30 = f32[8,128]{1,0:T(8,128)S(1)} collective-permute-done((f32[8,128]{1,0:T(8,128)S(1)}, f32[8,128]{1,0:T(8,128)S(1)}, u32[]{:S(2)}, u32[]{:S(2)}) %collective-permute-start.30) | collective-permute-done | bytes 4128 | tf_op jit(solution)/shard_map/ppermute | solution.py:34
  137.9 4.9 %shard_map.97 = (bf16[2,2048,256]{2,1,0:T(8,128)(2,1)S(1)}, bf16[2,256,256]{2,1,0:T(8,128)(2,1)S(1)}) custom-call(s32[2]{0:T(128)S(1)} %pad_add_fusion.at_ref, f32[8,128]{1,0:T(8,128)S(1)} %add_add_fusion.squares_ref, f32[2,2048,256]{2,1,0:T(8,128)S(1)} %get-tuple-element.33.grad_ref, f32[2,2048,256]{2,1,0:T(8,128)S(1)} %get-tuple-element.34.master_ref, ...), custom_call_target="tpu_custom_call" | custom-call | tf_op jit(solution)/shard_map/pallas_call | solution.py:263
  142.8 2.3 %shard_map.98 = (f32[2,256,256]{2,1,0:T(8,128)S(1)}, bf16[2,256,256]{2,1,0:T(8,128)(2,1)S(1)}, bf16[2,256,256]{2,1,0:T(8,128)(2,1)S(1)}) custom-call(s32[2]{0:T(128)S(1)} %pad_add_fusion.at_ref, bf16[2,2048,256]{2,1,0:T(8,128)(2,1)S(1)} %get-tuple-element.41.weight, bf16[256,512]{1,0:T(8,128)(2,1)S(1)} %get-tuple-element.42.refs_0_, ...), custom_call_target="tpu_custom_call" | custom-call | tf_op jit(solution)/shard_map/pallas_call | solution.py:271
  145.2 2.5 %collective-permute-start.43 = (bf16[2,256,256]{2,1,0:T(8,128)(2,1)S(1)}, bf16[2,256,256]{2,1,0:T(8,128)(2,1)S(1)}, u32[]{:S(2)}, u32[]{:S(2)}) collective-permute-start(bf16[2,256,256]{2,1,0:T(8,128)(2,1)S(1)} %get-tuple-element.51), channel_id=1, source_target_pairs={{0,12},{4,8},{8,4},{12,0},{1,13},{5,9},{9,5},{13,1},{2,14},{6,10},... | collective-permute-start | bytes 786440 | tf_op jit(solution)/shard_map/ppermute | solution.py:39
  147.7 0.9 collective-permute-start.42
  148.7 5.2 %shard_map.96 = (f32[2,2048,256]{2,1,0:T(8,128)}, f32[2,2048,256]{2,1,0:T(8,128)}, f32[2,2048,256]{2,1,0:T(8,128)}) custom-call(f32[8,128]{1,0:T(8,128)S(1)} %add_add_fusion.squares_ref, f32[2,2048,256]{2,1,0:T(8,128)S(1)} %get-tuple-element.33.grad_ref, f32[2,2048,256]{2,1,0:T(8,128)S(1)} %get-tuple-element.34.master_ref, ...), custom_call_target="tpu_custom_call" | custom-call | tf_op jit(solution)/shard_map/pallas_call | solution.py:282
  153.9 2.4 %collective-permute-done.41 = bf16[2,256,256]{2,1,0:T(8,128)(2,1)S(1)} collective-permute-done((bf16[2,256,256]{2,1,0:T(8,128)(2,1)S(1)}, bf16[2,256,256]{2,1,0:T(8,128)(2,1)S(1)}, u32[]{:S(2)}, u32[]{:S(2)}) %collective-permute-start.41) | collective-permute-done | bytes 262176 | tf_op jit(solution)/shard_map/ppermute | solution.py:39
  156.3 4.1 %collective-permute-done.43 = bf16[2,256,256]{2,1,0:T(8,128)(2,1)S(1)} collective-permute-done((bf16[2,256,256]{2,1,0:T(8,128)(2,1)S(1)}, bf16[2,256,256]{2,1,0:T(8,128)(2,1)S(1)}, u32[]{:S(2)}, u32[]{:S(2)}) %collective-permute-start.43) | collective-permute-done | bytes 262176 | tf_op jit(solution)/shard_map/ppermute | solution.py:39
  160.4 8.9 %collective-permute-done.42 = bf16[2,256,256]{2,1,0:T(8,128)(2,1)S(1)} collective-permute-done((bf16[2,256,256]{2,1,0:T(8,128)(2,1)S(1)}, bf16[2,256,256]{2,1,0:T(8,128)(2,1)S(1)}, u32[]{:S(2)}, u32[]{:S(2)}) %collective-permute-start.42) | collective-permute-done | bytes 262176 | tf_op jit(solution)/shard_map/ppermute | solution.py:39
  169.2 0.8 add_convert_fusion
  (43 shorter events, 0.8 us)
Async XLA Ops:
  0.6 7.1 %copy-start = (bf16[2,256,256]{2,1,0:T(8,128)(2,1)S(1)}, bf16[2,256,256]{2,1,0:T(8,128)(2,1)}, u32[]{:S(2)}) copy-start(bf16[2,256,256]{2,1,0:T(8,128)(2,1)} %refs_12_.1) | copy-start | bytes 786436
  2.0 15.2 %collective-permute-start.1 = (bf16[256,512]{1,0:T(8,128)(2,1)S(1)}, bf16[256,512]{1,0:T(8,128)(2,1)S(1)}, u32[]{:S(2)}, u32[]{:S(2)}) collective-permute-start(bf16[256,512]{1,0:T(8,128)(2,1)S(1)} %get-tuple-element.54), channel_id=1, source_target_pairs={{0,4},{4,0},{8,12},{12,8},{1,5},{5,1},{9,13},{13,9},{2,6},{6,2},{1... | collective-permute-start | bytes 786440 | tf_op jit(solution)/shard_map/ppermute | solution.py:39
  5.1 27.0 %collective-permute-start.3 = (bf16[256,512]{1,0:T(8,128)(2,1)S(1)}, bf16[256,512]{1,0:T(8,128)(2,1)S(1)}, u32[]{:S(2)}, u32[]{:S(2)}) collective-permute-start(bf16[256,512]{1,0:T(8,128)(2,1)S(1)} %get-tuple-element.53), channel_id=1, source_target_pairs={{0,8},{4,12},{8,0},{12,4},{1,9},{5,13},{9,1},{13,5},{2,10},{6,14},... | collective-permute-start | bytes 786440 | tf_op jit(solution)/shard_map/ppermute | solution.py:39
  7.7 31.9 %collective-permute-start.5 = (bf16[256,512]{1,0:T(8,128)(2,1)S(1)}, bf16[256,512]{1,0:T(8,128)(2,1)S(1)}, u32[]{:S(2)}, u32[]{:S(2)}) collective-permute-start(bf16[256,512]{1,0:T(8,128)(2,1)S(1)} %get-tuple-element.52), channel_id=1, source_target_pairs={{0,12},{4,8},{8,4},{12,0},{1,13},{5,9},{9,5},{13,1},{2,14},{6,10},... | collective-permute-start | bytes 786440 | tf_op jit(solution)/shard_map/ppermute | solution.py:39
  7.7 41.2 %collective-permute-start.16 = (bf16[2,256,256]{2,1,0:T(8,128)(2,1)S(1)}, bf16[2,256,256]{2,1,0:T(8,128)(2,1)S(1)}, u32[]{:S(2)}, u32[]{:S(2)}) collective-permute-start(bf16[2,256,256]{2,1,0:T(8,128)(2,1)S(1)} %copy-done), channel_id=1, source_target_pairs={{0,8},{4,12},{8,0},{12,4},{1,9},{5,13},{9,1},{13,5},{2,10},{6,14},... | collective-permute-start | bytes 786440 | tf_op jit(solution)/shard_map/ppermute | solution.py:39
  9.6 40.8 %collective-permute-start.14 = (bf16[2,256,256]{2,1,0:T(8,128)(2,1)S(1)}, bf16[2,256,256]{2,1,0:T(8,128)(2,1)S(1)}, u32[]{:S(2)}, u32[]{:S(2)}) collective-permute-start(bf16[2,256,256]{2,1,0:T(8,128)(2,1)S(1)} %copy-done), channel_id=1, source_target_pairs={{0,4},{4,0},{8,12},{12,8},{1,5},{5,1},{9,13},{13,9},{2,6},{6,2},{1... | collective-permute-start | bytes 786440 | tf_op jit(solution)/shard_map/ppermute | solution.py:39
  17.1 33.8 %collective-permute-start = (bf16[256,512]{1,0:T(8,128)(2,1)S(1)}, bf16[256,512]{1,0:T(8,128)(2,1)S(1)}, u32[]{:S(2)}, u32[]{:S(2)}) collective-permute-start(bf16[256,512]{1,0:T(8,128)(2,1)S(1)} %get-tuple-element.55), channel_id=1, source_target_pairs={{0,16},{16,0},{1,17},{17,1},{2,18},{18,2},{3,19},{19,3},{4,20},{20... | collective-permute-start | bytes 786440 | tf_op jit(solution)/shard_map/ppermute | solution.py:34
  32.1 20.4 %collective-permute-start.13 = (bf16[2,256,256]{2,1,0:T(8,128)(2,1)S(1)}, bf16[2,256,256]{2,1,0:T(8,128)(2,1)S(1)}, u32[]{:S(2)}, u32[]{:S(2)}) collective-permute-start(bf16[2,256,256]{2,1,0:T(8,128)(2,1)S(1)} %copy-done), channel_id=1, source_target_pairs={{0,16},{16,0},{1,17},{17,1},{2,18},{18,2},{3,19},{19,3},{4,20},{20... | collective-permute-start | bytes 786440 | tf_op jit(solution)/shard_map/ppermute | solution.py:34
  39.6 13.6 %collective-permute-start.31 = (bf16[256,512]{1,0:T(8,128)(2,1)S(1)}, bf16[256,512]{1,0:T(8,128)(2,1)S(1)}, u32[]{:S(2)}, u32[]{:S(2)}) collective-permute-start(bf16[256,512]{1,0:T(8,128)(2,1)S(1)} %get-tuple-element.40), channel_id=1, source_target_pairs={{0,8},{4,12},{8,0},{12,4},{1,9},{5,13},{9,1},{13,5},{2,10},{6,14},... | collective-permute-start | bytes 786440 | tf_op jit(solution)/shard_map/ppermute | solution.py:39
  48.9 9.2 %collective-permute-start.4 = (bf16[256,512]{1,0:T(8,128)(2,1)S(1)}, bf16[256,512]{1,0:T(8,128)(2,1)S(1)}, u32[]{:S(2)}, u32[]{:S(2)}) collective-permute-start(bf16[256,512]{1,0:T(8,128)(2,1)S(1)} %collective-permute-done.3.refs_2_), channel_id=1, source_target_pairs={{0,16},{16,0},{1,17},{17,1},{2,18},{18,2},{3,19},{19,3},{4,20},{20... | collective-permute-start | bytes 786440 | tf_op jit(solution)/shard_map/ppermute | solution.py:34
  50.4 12.3 %collective-permute-start.6 = (bf16[256,512]{1,0:T(8,128)(2,1)S(1)}, bf16[256,512]{1,0:T(8,128)(2,1)S(1)}, u32[]{:S(2)}, u32[]{:S(2)}) collective-permute-start(bf16[256,512]{1,0:T(8,128)(2,1)S(1)} %collective-permute-done.5.refs_3_), channel_id=1, source_target_pairs={{0,16},{16,0},{1,17},{17,1},{2,18},{18,2},{3,19},{19,3},{4,20},{20... | collective-permute-start | bytes 786440 | tf_op jit(solution)/shard_map/ppermute | solution.py:34
  51.0 14.6 %collective-permute-start.2 = (bf16[256,512]{1,0:T(8,128)(2,1)S(1)}, bf16[256,512]{1,0:T(8,128)(2,1)S(1)}, u32[]{:S(2)}, u32[]{:S(2)}) collective-permute-start(bf16[256,512]{1,0:T(8,128)(2,1)S(1)} %collective-permute-done.1.refs_1_), channel_id=1, source_target_pairs={{0,16},{16,0},{1,17},{17,1},{2,18},{18,2},{3,19},{19,3},{4,20},{20... | collective-permute-start | bytes 786440 | tf_op jit(solution)/shard_map/ppermute | solution.py:34
  52.5 14.5 %collective-permute-start.35 = (bf16[256,512]{1,0:T(8,128)(2,1)S(1)}, bf16[256,512]{1,0:T(8,128)(2,1)S(1)}, u32[]{:S(2)}, u32[]{:S(2)}) collective-permute-start(bf16[256,512]{1,0:T(8,128)(2,1)S(1)} %get-tuple-element.43), channel_id=1, source_target_pairs={{0,4},{4,0},{8,12},{12,8},{1,5},{5,1},{9,13},{13,9},{2,6},{6,2},{1... | collective-permute-start | bytes 786440 | tf_op jit(solution)/shard_map/ppermute | solution.py:39
  53.3 16.4 %collective-permute-start.8 = (bf16[256,512]{1,0:T(8,128)(2,1)S(1)}, bf16[256,512]{1,0:T(8,128)(2,1)S(1)}, u32[]{:S(2)}, u32[]{:S(2)}) collective-permute-start(bf16[256,512]{1,0:T(8,128)(2,1)S(1)} %collective-permute-done.refs_0_), channel_id=1, source_target_pairs={{0,2},{1,3},{2,0},{3,1},{4,6},{5,7},{6,4},{7,5},{8,10},{9,11},{10,... | collective-permute-start | bytes 786440 | tf_op jit(solution)/shard_map/ppermute | solution.py:52
  58.1 12.2 %collective-permute-start.10 = (bf16[256,512]{1,0:T(8,128)(2,1)S(1)}, bf16[256,512]{1,0:T(8,128)(2,1)S(1)}, u32[]{:S(2)}, u32[]{:S(2)}) collective-permute-start(bf16[256,512]{1,0:T(8,128)(2,1)S(1)} %collective-permute-done.4.refs_2_), channel_id=1, source_target_pairs={{0,2},{1,3},{2,0},{3,1},{4,6},{5,7},{6,4},{7,5},{8,10},{9,11},{10,... | collective-permute-start | bytes 786440 | tf_op jit(solution)/shard_map/ppermute | solution.py:52
  62.7 11.0 %collective-permute-start.11 = (bf16[256,512]{1,0:T(8,128)(2,1)S(1)}, bf16[256,512]{1,0:T(8,128)(2,1)S(1)}, u32[]{:S(2)}, u32[]{:S(2)}) collective-permute-start(bf16[256,512]{1,0:T(8,128)(2,1)S(1)} %collective-permute-done.6.refs_3_), channel_id=1, source_target_pairs={{0,2},{1,3},{2,0},{3,1},{4,6},{5,7},{6,4},{7,5},{8,10},{9,11},{10,... | collective-permute-start | bytes 786440 | tf_op jit(solution)/shard_map/ppermute | solution.py:52
  65.5 13.8 %collective-permute-start.9 = (bf16[256,512]{1,0:T(8,128)(2,1)S(1)}, bf16[256,512]{1,0:T(8,128)(2,1)S(1)}, u32[]{:S(2)}, u32[]{:S(2)}) collective-permute-start(bf16[256,512]{1,0:T(8,128)(2,1)S(1)} %collective-permute-done.2.refs_1_), channel_id=1, source_target_pairs={{0,2},{1,3},{2,0},{3,1},{4,6},{5,7},{6,4},{7,5},{8,10},{9,11},{10,... | collective-permute-start | bytes 786440 | tf_op jit(solution)/shard_map/ppermute | solution.py:52
  67.0 13.7 %collective-permute-start.36 = (bf16[256,512]{1,0:T(8,128)(2,1)S(1)}, bf16[256,512]{1,0:T(8,128)(2,1)S(1)}, u32[]{:S(2)}, u32[]{:S(2)}) collective-permute-start(bf16[256,512]{1,0:T(8,128)(2,1)S(1)} %get-tuple-element.44), channel_id=1, source_target_pairs={{0,12},{4,8},{8,4},{12,0},{1,13},{5,9},{9,5},{13,1},{2,14},{6,10},... | collective-permute-start | bytes 786440 | tf_op jit(solution)/shard_map/ppermute | solution.py:39
  69.7 15.2 %collective-permute-start.21 = (bf16[256,512]{1,0:T(8,128)(2,1)S(1)}, bf16[256,512]{1,0:T(8,128)(2,1)S(1)}, u32[]{:S(2)}, u32[]{:S(2)}) collective-permute-start(bf16[256,512]{1,0:T(8,128)(2,1)S(1)} %collective-permute-done.1.refs_1_), channel_id=1, source_target_pairs={{0,2},{1,3},{2,0},{3,1},{4,6},{5,7},{6,4},{7,5},{8,10},{9,11},{10,... | collective-permute-start | bytes 786440 | tf_op jit(solution)/shard_map/ppermute | solution.py:52
  70.3 20.3 %collective-permute-start.22 = (bf16[256,512]{1,0:T(8,128)(2,1)S(1)}, bf16[256,512]{1,0:T(8,128)(2,1)S(1)}, u32[]{:S(2)}, u32[]{:S(2)}) collective-permute-start(bf16[256,512]{1,0:T(8,128)(2,1)S(1)} %collective-permute-done.3.refs_2_), channel_id=1, source_target_pairs={{0,2},{1,3},{2,0},{3,1},{4,6},{5,7},{6,4},{7,5},{8,10},{9,11},{10,... | collective-permute-start | bytes 786440 | tf_op jit(solution)/shard_map/ppermute | solution.py:52
  73.7 22.5 %collective-permute-start.23 = (bf16[256,512]{1,0:T(8,128)(2,1)S(1)}, bf16[256,512]{1,0:T(8,128)(2,1)S(1)}, u32[]{:S(2)}, u32[]{:S(2)}) collective-permute-start(bf16[256,512]{1,0:T(8,128)(2,1)S(1)} %collective-permute-done.5.refs_3_), channel_id=1, source_target_pairs={{0,2},{1,3},{2,0},{3,1},{4,6},{5,7},{6,4},{7,5},{8,10},{9,11},{10,... | collective-permute-start | bytes 786440 | tf_op jit(solution)/shard_map/ppermute | solution.py:52
  79.3 16.9 %collective-permute-start.18 = (bf16[2,256,256]{2,1,0:T(8,128)(2,1)S(1)}, bf16[2,256,256]{2,1,0:T(8,128)(2,1)S(1)}, u32[]{:S(2)}, u32[]{:S(2)}) collective-permute-start(bf16[2,256,256]{2,1,0:T(8,128)(2,1)S(1)} %collective-permute-done.16.refs_14_), channel_id=1, source_target_pairs={{0,4},{4,0},{8,12},{12,8},{1,5},{5,1},{9,13},{13,9},{2,6},{6,2},{1... | collective-permute-start | bytes 786440 | tf_op jit(solution)/shard_map/ppermute | solution.py:39
  80.7 16.1 %collective-permute-start.17 = (bf16[2,256,256]{2,1,0:T(8,128)(2,1)S(1)}, bf16[2,256,256]{2,1,0:T(8,128)(2,1)S(1)}, u32[]{:S(2)}, u32[]{:S(2)}) collective-permute-start(bf16[2,256,256]{2,1,0:T(8,128)(2,1)S(1)} %collective-permute-done.16.refs_14_), channel_id=1, source_target_pairs={{0,16},{16,0},{1,17},{17,1},{2,18},{18,2},{3,19},{19,3},{4,20},{20... | collective-permute-start | bytes 786440 | tf_op jit(solution)/shard_map/ppermute | solution.py:34
  84.9 12.0 %collective-permute-start.15 = (bf16[2,256,256]{2,1,0:T(8,128)(2,1)S(1)}, bf16[2,256,256]{2,1,0:T(8,128)(2,1)S(1)}, u32[]{:S(2)}, u32[]{:S(2)}) collective-permute-start(bf16[2,256,256]{2,1,0:T(8,128)(2,1)S(1)} %collective-permute-done.14.refs_13_), channel_id=1, source_target_pairs={{0,16},{16,0},{1,17},{17,1},{2,18},{18,2},{3,19},{19,3},{4,20},{20... | collective-permute-start | bytes 786440 | tf_op jit(solution)/shard_map/ppermute | solution.py:34
  90.5 8.9 %collective-permute-start.38 = (bf16[256,512]{1,0:T(8,128)(2,1)S(1)}, bf16[256,512]{1,0:T(8,128)(2,1)S(1)}, u32[]{:S(2)}, u32[]{:S(2)}) collective-permute-start(bf16[256,512]{1,0:T(8,128)(2,1)S(1)} %collective-permute-done.35.refs_1_), channel_id=1, source_target_pairs={{0,2},{1,3},{2,0},{3,1},{4,6},{5,7},{6,4},{7,5},{8,10},{9,11},{10,... | collective-permute-start | bytes 786440 | tf_op jit(solution)/shard_map/ppermute | solution.py:52
  96.2 21.1 %collective-permute-start.7 = (bf16[1024,512]{1,0:T(8,128)(2,1)S(1)}, bf16[1024,512]{1,0:T(8,128)(2,1)S(1)}, u32[]{:S(2)}, u32[]{:S(2)}) collective-permute-start(bf16[1024,512]{1,0:T(8,128)(2,1)S(1)} %pad_maximum_fusion), channel_id=1, source_target_pairs={{0,1},{1,0},{2,3},{3,2},{4,5},{5,4},{6,7},{7,6},{8,9},{9,8},{10,11... | collective-permute-start | bytes 3145736 | tf_op jit(solution)/shard_map/ppermute | solution.py:52
  96.2 21.1 %collective-permute-start.12 = (bf16[1024,512]{1,0:T(8,128)(2,1)S(1)}, bf16[1024,512]{1,0:T(8,128)(2,1)S(1)}, u32[]{:S(2)}, u32[]{:S(2)}) collective-permute-start(bf16[1024,512]{1,0:T(8,128)(2,1)S(1)} %pad_maximum_fusion.1), channel_id=1, source_target_pairs={{0,1},{1,0},{2,3},{3,2},{4,5},{5,4},{6,7},{7,6},{8,9},{9,8},{10,11... | collective-permute-start | bytes 3145736 | tf_op jit(solution)/shard_map/ppermute | solution.py:52
  96.8 17.0 %collective-permute-start.20 = (bf16[768,512]{1,0:T(8,128)(2,1)S(1)}, bf16[768,512]{1,0:T(8,128)(2,1)S(1)}, u32[]{:S(2)}, u32[]{:S(2)}) collective-permute-start(bf16[768,512]{1,0:T(8,128)(2,1)S(1)} %pad_maximum_fusion.2), channel_id=1, source_target_pairs={{0,1},{1,0},{2,3},{3,2},{4,5},{5,4},{6,7},{7,6},{8,9},{9,8},{10,11... | collective-permute-start | bytes 2359304 | tf_op jit(solution)/shard_map/ppermute | solution.py:52
  96.9 17.0 %collective-permute-start.24 = (bf16[768,512]{1,0:T(8,128)(2,1)S(1)}, bf16[768,512]{1,0:T(8,128)(2,1)S(1)}, u32[]{:S(2)}, u32[]{:S(2)}) collective-permute-start(bf16[768,512]{1,0:T(8,128)(2,1)S(1)} %pad_maximum_fusion.3), channel_id=1, source_target_pairs={{0,1},{1,0},{2,3},{3,2},{4,5},{5,4},{6,7},{7,6},{8,9},{9,8},{10,11... | collective-permute-start | bytes 2359304 | tf_op jit(solution)/shard_map/ppermute | solution.py:52
  99.4 6.4 %collective-permute-start.39 = (bf16[256,512]{1,0:T(8,128)(2,1)S(1)}, bf16[256,512]{1,0:T(8,128)(2,1)S(1)}, u32[]{:S(2)}, u32[]{:S(2)}) collective-permute-start(bf16[256,512]{1,0:T(8,128)(2,1)S(1)} %collective-permute-done.36.refs_2_), channel_id=1, source_target_pairs={{0,2},{1,3},{2,0},{3,1},{4,6},{5,7},{6,4},{7,5},{8,10},{9,11},{10,... | collective-permute-start | bytes 786440 | tf_op jit(solution)/shard_map/ppermute | solution.py:52
  105.8 6.4 %collective-permute-start.19 = (bf16[2,256,256]{2,1,0:T(8,128)(2,1)S(1)}, bf16[2,256,256]{2,1,0:T(8,128)(2,1)S(1)}, u32[]{:S(2)}, u32[]{:S(2)}) collective-permute-start(bf16[2,256,256]{2,1,0:T(8,128)(2,1)S(1)} %collective-permute-done.18.refs_15_), channel_id=1, source_target_pairs={{0,16},{16,0},{1,17},{17,1},{2,18},{18,2},{3,19},{19,3},{4,20},{20... | collective-permute-start | bytes 786440 | tf_op jit(solution)/shard_map/ppermute | solution.py:34
  112.2 9.0 %collective-permute-start.33 = (bf16[256,512]{1,0:T(8,128)(2,1)S(1)}, bf16[256,512]{1,0:T(8,128)(2,1)S(1)}, u32[]{:S(2)}, u32[]{:S(2)}) collective-permute-start(bf16[256,512]{1,0:T(8,128)(2,1)S(1)} %collective-permute-done.31.refs_0_), channel_id=1, source_target_pairs={{0,2},{1,3},{2,0},{3,1},{4,6},{5,7},{6,4},{7,5},{8,10},{9,11},{10,... | collective-permute-start | bytes 786440 | tf_op jit(solution)/shard_map/ppermute | solution.py:52
  113.8 29.0 %collective-permute-start.37 = (bf16[512,512]{1,0:T(8,128)(2,1)S(1)}, bf16[512,512]{1,0:T(8,128)(2,1)S(1)}, u32[]{:S(2)}, u32[]{:S(2)}) collective-permute-start(bf16[512,512]{1,0:T(8,128)(2,1)S(1)} %pad_maximum_fusion.4), channel_id=1, source_target_pairs={{0,1},{1,0},{2,3},{3,2},{4,5},{5,4},{6,7},{7,6},{8,9},{9,8},{10,11... | collective-permute-start | bytes 1572872 | tf_op jit(solution)/shard_map/ppermute | solution.py:52
  113.9 28.9 %collective-permute-start.40 = (bf16[512,512]{1,0:T(8,128)(2,1)S(1)}, bf16[512,512]{1,0:T(8,128)(2,1)S(1)}, u32[]{:S(2)}, u32[]{:S(2)}) collective-permute-start(bf16[512,512]{1,0:T(8,128)(2,1)S(1)} %pad_maximum_fusion.5), channel_id=1, source_target_pairs={{0,1},{1,0},{2,3},{3,2},{4,5},{5,4},{6,7},{7,6},{8,9},{9,8},{10,11... | collective-permute-start | bytes 1572872 | tf_op jit(solution)/shard_map/ppermute | solution.py:52
  120.5 3.1 %collective-permute-start.25 = (f32[8,128]{1,0:T(8,128)S(1)}, f32[8,128]{1,0:T(8,128)S(1)}, u32[]{:S(2)}, u32[]{:S(2)}) collective-permute-start(f32[8,128]{1,0:T(8,128)S(1)} %get-tuple-element.32), channel_id=1, source_target_pairs={{0,1},{1,2},{2,3},{3,0},{4,5},{5,6},{6,7},{7,4},{8,9},{9,10},{10,1... | collective-permute-start | bytes 12296 | tf_op jit(solution)/shard_map/ppermute | solution.py:34
  120.7 3.6 %collective-permute-start.26 = (f32[8,128]{1,0:T(8,128)S(1)}, f32[8,128]{1,0:T(8,128)S(1)}, u32[]{:S(2)}, u32[]{:S(2)}) collective-permute-start(f32[8,128]{1,0:T(8,128)S(1)} %get-tuple-element.32), channel_id=1, source_target_pairs={{0,2},{1,3},{2,0},{3,1},{4,6},{5,7},{6,4},{7,5},{8,10},{9,11},{10,... | collective-permute-start | bytes 12296 | tf_op jit(solution)/shard_map/ppermute | solution.py:34
  121.2 3.1 %collective-permute-start.27 = (f32[8,128]{1,0:T(8,128)S(1)}, f32[8,128]{1,0:T(8,128)S(1)}, u32[]{:S(2)}, u32[]{:S(2)}) collective-permute-start(f32[8,128]{1,0:T(8,128)S(1)} %get-tuple-element.32), channel_id=1, source_target_pairs={{0,3},{1,0},{2,1},{3,2},{4,7},{5,4},{6,5},{7,6},{8,11},{9,8},{10,9... | collective-permute-start | bytes 12296 | tf_op jit(solution)/shard_map/ppermute | solution.py:34
  123.6 14.3 %collective-permute-start.32 = (bf16[256,512]{1,0:T(8,128)(2,1)S(1)}, bf16[256,512]{1,0:T(8,128)(2,1)S(1)}, u32[]{:S(2)}, u32[]{:S(2)}) collective-permute-start(bf16[256,512]{1,0:T(8,128)(2,1)S(1)} %collective-permute-done.31.refs_0_), channel_id=1, source_target_pairs={{0,1},{1,0},{2,3},{3,2},{4,5},{5,4},{6,7},{7,6},{8,9},{9,8},{10,11... | collective-permute-start | bytes 786440 | tf_op jit(solution)/shard_map/ppermute | solution.py:52
  124.3 13.6 %collective-permute-start.34 = (bf16[256,512]{1,0:T(8,128)(2,1)S(1)}, bf16[256,512]{1,0:T(8,128)(2,1)S(1)}, u32[]{:S(2)}, u32[]{:S(2)}) collective-permute-start(bf16[256,512]{1,0:T(8,128)(2,1)S(1)} %collective-permute-done.33.refs_2_), channel_id=1, source_target_pairs={{0,1},{1,0},{2,3},{3,2},{4,5},{5,4},{6,7},{7,6},{8,9},{9,8},{10,11... | collective-permute-start | bytes 786440 | tf_op jit(solution)/shard_map/ppermute | solution.py:52
  124.3 5.5 %collective-permute-start.28 = (f32[8,128]{1,0:T(8,128)S(1)}, f32[8,128]{1,0:T(8,128)S(1)}, u32[]{:S(2)}, u32[]{:S(2)}) collective-permute-start(f32[8,128]{1,0:T(8,128)S(1)} %add_add_fusion.1), channel_id=1, source_target_pairs={{0,4},{4,8},{8,12},{12,0},{1,5},{5,9},{9,13},{13,1},{2,6},{6,10},{... | collective-permute-start | bytes 12296 | tf_op jit(solution)/shard_map/ppermute | solution.py:34
  129.7 4.5 %collective-permute-start.29 = (f32[8,128]{1,0:T(8,128)S(1)}, f32[8,128]{1,0:T(8,128)S(1)}, u32[]{:S(2)}, u32[]{:S(2)}) collective-permute-start(f32[8,128]{1,0:T(8,128)S(1)} %add_add_fusion.1), channel_id=1, source_target_pairs={{0,8},{4,12},{8,0},{12,4},{1,9},{5,13},{9,1},{13,5},{2,10},{6,14},... | collective-permute-start | bytes 12296 | tf_op jit(solution)/shard_map/ppermute | solution.py:34
  134.2 3.6 %collective-permute-start.30 = (f32[8,128]{1,0:T(8,128)S(1)}, f32[8,128]{1,0:T(8,128)S(1)}, u32[]{:S(2)}, u32[]{:S(2)}) collective-permute-start(f32[8,128]{1,0:T(8,128)S(1)} %add_add_fusion.1), channel_id=1, source_target_pairs={{0,12},{4,0},{8,4},{12,8},{1,13},{5,1},{9,5},{13,9},{2,14},{6,2},{... | collective-permute-start | bytes 12296 | tf_op jit(solution)/shard_map/ppermute | solution.py:34
  145.1 11.2 %collective-permute-start.41 = (bf16[2,256,256]{2,1,0:T(8,128)(2,1)S(1)}, bf16[2,256,256]{2,1,0:T(8,128)(2,1)S(1)}, u32[]{:S(2)}, u32[]{:S(2)}) collective-permute-start(bf16[2,256,256]{2,1,0:T(8,128)(2,1)S(1)} %get-tuple-element.49), channel_id=1, source_target_pairs={{0,4},{4,0},{8,12},{12,8},{1,5},{5,1},{9,13},{13,9},{2,6},{6,2},{1... | collective-permute-start | bytes 786440 | tf_op jit(solution)/shard_map/ppermute | solution.py:39
  145.2 15.2 %collective-permute-start.43 = (bf16[2,256,256]{2,1,0:T(8,128)(2,1)S(1)}, bf16[2,256,256]{2,1,0:T(8,128)(2,1)S(1)}, u32[]{:S(2)}, u32[]{:S(2)}) collective-permute-start(bf16[2,256,256]{2,1,0:T(8,128)(2,1)S(1)} %get-tuple-element.51), channel_id=1, source_target_pairs={{0,12},{4,8},{8,4},{12,0},{1,13},{5,9},{9,5},{13,1},{2,14},{6,10},... | collective-permute-start | bytes 786440 | tf_op jit(solution)/shard_map/ppermute | solution.py:39
  147.7 21.5 %collective-permute-start.42 = (bf16[2,256,256]{2,1,0:T(8,128)(2,1)S(1)}, bf16[2,256,256]{2,1,0:T(8,128)(2,1)S(1)}, u32[]{:S(2)}, u32[]{:S(2)}) collective-permute-start(bf16[2,256,256]{2,1,0:T(8,128)(2,1)S(1)} %get-tuple-element.50), channel_id=1, source_target_pairs={{0,8},{4,12},{8,0},{12,4},{1,9},{5,13},{9,1},{13,5},{2,10},{6,14},... | collective-permute-start | bytes 786440 | tf_op jit(solution)/shard_map/ppermute | solution.py:39
